TPU v7x, 32 devices: a whole 2x2x4 slice. The times are simulated.
32 devices in a mesh: dp: 4 (over z), ctx: 2 (over y), tp: 4 (over x, core).
Axes of the slice: x: 2, y: 2, z: 4, core: 2. Of those that a mesh axis runs over, the one named last changes fastest.
Arguments:
- queries: bfloat16 [1536, 4096], P(('dp', 'ctx'), 'tp'), parts along dimension 0, may hold values from -40 to 40
- keys: bfloat16 [1536, 512], P(('dp', 'ctx'), 'tp'), parts along dimension 0, may hold values from -4 to 4
- values: bfloat16 [1536, 512], P(('dp', 'ctx'), 'tp'), parts along dimension 0, may hold values from -6 to 6
- grad_out: bfloat16 [1536, 4096], P(('dp', 'ctx'), 'tp'), parts along dimension 0, may hold values from -6 to 6
- segments: int32 [1536], P(('dp', 'ctx')), parts along dimension 0, may hold values from 0 to 5, never falling along the last dimension, each value on 1 to 288 neighbouring positions
- sinks: float32 [64], P('tp'), may hold values from -1 to 5
Outputs:
- grad_queries: bfloat16 [1536, 4096], P(('dp', 'ctx'), 'tp'), parts along dimension 0
- keys_gradient: bfloat16 [1536, 512], P(('dp', 'ctx'), 'tp'), parts along dimension 0
- values_gradient: bfloat16 [1536, 512], P(('dp', 'ctx'), 'tp'), parts along dimension 0
- grad_sinks: float32 [256], P(('dp', 'tp')), parts along dimension 0
There are 4 independent parts, one for each index of `dp`. A program takes and returns all parts, laid end to end along the dimension named above; an argument that names none is the same for every part. Nothing has to cross between parts.
All inputs are finite; a program needn't handle non-finite values.
Results may differ from a plain program's by a relative error of at most 0.012.
The roundings to bfloat16 on the way count: a program that leaves them out, or rounds other values in their place, can miss the bound.
Values may be sent and summed in bfloat16 or wider, within the bound.
No kernel may reach another device: no remote copies, remote signals or barrier semaphores. Data moves between devices by JAX's collectives and lax.ppermute only.
A program may use at most 64 MiB of HBM per device.

v0:
```python
import jax
import jax.numpy as jnp
from jax import lax
from jax.sharding import PartitionSpec as P

HEAD_SIZE = 64


NEG_FILL = -1e30


def head_major(block, kv_heads):
    length = block.shape[0]
    query_group = block.shape[1] // (kv_heads * HEAD_SIZE)
    return (
        block.reshape(length, kv_heads, query_group, HEAD_SIZE)
        .transpose(1, 2, 0, 3)
        .reshape(kv_heads, query_group * length, HEAD_SIZE)
    )


def row_major(stacked, length):
    kv_heads = stacked.shape[0]
    query_group = stacked.shape[1] // length
    return (
        stacked.reshape(kv_heads, query_group, length, HEAD_SIZE)
        .transpose(2, 0, 1, 3)
        .reshape(length, kv_heads * query_group * HEAD_SIZE)
    )


def add_rows(buffer, term, start):
    length = term.shape[1]
    flat = term.transpose(1, 0, 2).reshape(length, term.shape[0] * HEAD_SIZE)
    before = lax.dynamic_slice_in_dim(buffer, start, length, 0)
    return lax.dynamic_update_slice_in_dim(buffer, before + flat, start, 0)


def on_device(queries, keys, values, grad_out, segments, sinks):
    length = queries.shape[0]
    kv_heads = keys.shape[1] // HEAD_SIZE
    query_group = queries.shape[1] // keys.shape[1]
    scale = HEAD_SIZE ** (-0.5)
    place = lax.axis_index("ctx")
    key_all, value_all = (
        lax.all_gather(keys, "ctx", axis=0, tiled=True),
        lax.all_gather(values, "ctx", axis=0, tiled=True),
    )
    seg_all = lax.all_gather(segments, "ctx", axis=0, tiled=True)
    total_sum = key_all.shape[0]
    key_heads = key_all.reshape(total_sum, kv_heads, HEAD_SIZE).transpose(1, 0, 2)
    value_heads = value_all.reshape(total_sum, kv_heads, HEAD_SIZE).transpose(1, 0, 2)

    def tile_scores(query_heads, query_seg, query_first, tile):
        start = tile * length
        key_block = lax.dynamic_slice_in_dim(key_heads, start, length, 1)
        value_block = lax.dynamic_slice_in_dim(value_heads, start, length, 1)
        raw = (
            lax.dot_general(
                query_heads,
                key_block,
                (((2,), (2,)), ((0,), (0,))),
                preferred_element_type=jnp.float32,
            )
            * scale
        )
        key_seg = lax.dynamic_slice_in_dim(seg_all, start, length, 0)
        query_pos = query_first + lax.iota(jnp.int32, length)
        key_pos = start + lax.iota(jnp.int32, length)
        allowed = (key_pos[None, :] <= query_pos[:, None]) & (
            key_seg[None, :] == query_seg[:, None]
        )
        allowed = jnp.tile(allowed, (query_group, 1))[None]
        return (raw, allowed, key_block, value_block)

    home_q = head_major(queries, kv_heads)
    home_grad = head_major(grad_out, kv_heads)
    first = place * length
    row_shape = (kv_heads, query_group * length)
    sink_rows = jnp.broadcast_to(
        sinks.reshape(kv_heads, query_group, 1), (kv_heads, query_group, length)
    ).reshape(row_shape)

    def stat_step(tile, carry):
        top, mass = carry
        raw, allowed, key_block, value_block = tile_scores(home_q, segments, first, tile)
        masked = jnp.where(allowed, raw, NEG_FILL)
        new_top = jnp.maximum(top, jnp.max(masked, axis=-1))
        weight = jnp.where(allowed, jnp.exp(raw - new_top[..., None]), 0.0)
        mass = mass * jnp.exp(top - new_top) + jnp.sum(weight, axis=-1)
        return (new_top, mass)

    top, mass = lax.fori_loop(
        0, place + 1, stat_step, (sink_rows, jnp.ones(row_shape, jnp.float32))
    )
    lse_rows = top + jnp.log(mass)

    def out_step(tile, total_out):
        raw, allowed, key_block, value_block = tile_scores(home_q, segments, first, tile)
        prob_half = jnp.where(allowed, jnp.exp(raw - lse_rows[..., None]), 0.0).astype(jnp.bfloat16)
        return total_out + lax.dot_general(
            prob_half, value_block, (((2,), (1,)), ((0,), (0,))), preferred_element_type=jnp.float32
        )

    out = lax.fori_loop(0, place + 1, out_step, jnp.zeros(home_q.shape, jnp.float32))
    delta_rows = jnp.sum(home_grad.astype(jnp.float32) * out, axis=-1)
    stats = jnp.stack([lse_rows, delta_rows])
    sink_term = -jnp.sum(
        (jnp.exp(sink_rows - lse_rows) * delta_rows).reshape(kv_heads, query_group, length), axis=-1
    ).reshape(kv_heads * query_group)
    grad_sinks = lax.psum(sink_term, "ctx")
    buffers = (
        jnp.zeros((total_sum, kv_heads * HEAD_SIZE), jnp.float32),
        jnp.zeros((total_sum, kv_heads * HEAD_SIZE), jnp.float32),
    )
    home_low = 0
    stat_lse = stats[0]
    stat_delta = stats[1]

    def step(tile, carry):
        grad_acc, key_buf, value_buf = carry
        raw, allowed, key_block, value_block = tile_scores(home_q, segments, first, tile)
        prob = jnp.where(allowed, jnp.exp(raw - stat_lse[..., None]), 0.0)
        prob_half = prob.astype(jnp.bfloat16)
        dprob = lax.dot_general(
            home_grad, value_block, (((2,), (2,)), ((0,), (0,))), preferred_element_type=jnp.float32
        )
        dscore = (prob * (dprob - stat_delta[..., None])).astype(jnp.bfloat16)
        grad_acc = (
            grad_acc
            + lax.dot_general(
                dscore, key_block, (((2,), (1,)), ((0,), (0,))), preferred_element_type=jnp.float32
            )
            * scale
        )
        key_term = (
            lax.dot_general(
                dscore, home_q, (((1,), (1,)), ((0,), (0,))), preferred_element_type=jnp.float32
            )
            * scale
        )
        value_term = lax.dot_general(
            prob_half, home_grad, (((1,), (1,)), ((0,), (0,))), preferred_element_type=jnp.float32
        )
        key_buf = add_rows(key_buf, key_term, tile * length)
        value_buf = add_rows(value_buf, value_term, tile * length)
        return (grad_acc, key_buf, value_buf)

    start_acc = jnp.zeros(home_q.shape, jnp.float32)
    grad_home, key_buf, value_buf = lax.fori_loop(
        home_low, place + 1, step, (start_acc, buffers[0], buffers[1])
    )
    grad_rows = row_major(grad_home, length)
    key_own, value_own = (
        lax.psum_scatter(key_buf, "ctx", scatter_dimension=0, tiled=True),
        lax.psum_scatter(value_buf, "ctx", scatter_dimension=0, tiled=True),
    )
    return (
        grad_rows.astype(jnp.bfloat16),
        key_own.astype(jnp.bfloat16),
        value_own.astype(jnp.bfloat16),
        grad_sinks,
    )


def solution(mesh):
    placed = (
        P(("dp", "ctx"), "tp"),
        P(("dp", "ctx"), "tp"),
        P(("dp", "ctx"), "tp"),
        P(("dp", "ctx"), "tp"),
        P(("dp", "ctx")),
        P("tp"),
    )
    return jax.shard_map(
        on_device,
        mesh=mesh,
        in_specs=placed,
        out_specs=(
            P(("dp", "ctx"), "tp"),
            P(("dp", "ctx"), "tp"),
            P(("dp", "ctx"), "tp"),
            P(("dp", "tp")),
        ),
        check_vma=False,
    )
```

profile of v0, /device:TPU:0, one launch (start us, length us, event | category | flops | bytes accessed | tf_op | source)
XLA Modules:
  0.0 123.8 jit_solution(12425154984097969263)
XLA Ops:
  7.2 1.2 %dynamic-slice = u32[1]{0:T(128)} dynamic-slice(u32[32]{0:T(128)} %constant.62, u32[]{:T(128)S(6)} %add.118), dynamic_slice_sizes={1} | dynamic-slice | bytes 12
  9.2 0.9 dynamic-update-slice
  10.0 5.2 %all-reduce = s32[384]{0:T(512)S(1)} all-reduce(s32[384]{0:T(512)S(1)} %dynamic-update-slice), channel_id=1, replica_groups=mesh['dp'=4,'ctx'=2,'tp'=4] {'ctx'}, use_global_device_ids=true, to_apply=%add | all-reduce | flops 384 | bytes 3072
  15.3 1.2 copy.30
  16.5 0.3 copy.31
  16.8 1.2 reshape.250
  18.0 4.7 %all_gather.10 = bf16[384,128]{1,0:T(8,128)(2,1)S(1)} all-gather(bf16[192,128]{1,0:T(8,128)(2,1)S(1)} %copy-done.8), channel_id=1, replica_groups=mesh['dp'=4,'ctx'=2,'tp'=4] {'ctx'}, dimensions={0}, use_global_device_ids=true | all-gather | bytes 147456 | tf_op jit(solution)/shard_map/all_gather | solution.py:46
  22.7 0.7 copy.29
  23.4 0.1 broadcast_in_dim.58
  23.6 0.1 reshape.251
  23.7 0.6 copy-done.6
  24.3 3.5 %while.36 = (s32[]{:T(128)}, f32[2,1536]{1,0:T(2,128)S(1)}, f32[2,1536]{1,0:T(2,128)S(1)}, s32[]{:T(128)}, s32[]{:T(128)}, /*index=5*/s32[384]{0:T(512)S(1)}, s3...) while((s32[]{:T(128)}, f32[2,1536]{1,0:T(2,128)S(1)}, ...), condition=%wide.region_3.4_spmd, body=%wide.region_0.3_spmd.sunk | while | flops 79153544 | bytes 6891707 | solution.py:93
  24.4 0.1 compare_and_fusion.6
  24.5 0.2 tile.33
  24.7 0.7 tile.34
  25.4 1.8 %select_reduce_fusion.4 = (f32[2,1536]{1,0:T(2,128)S(1)}, f32[2,1536,192]{1,2,0:T(8,128)S(1)}) fusion(pred[1536,192]{0,1:T(8,128)(4,1)S(1)} %tile.34, bf16[2,1536,64]{1,2,0:T(8,128)(2,1)} %get-tuple-element.543, bf16[2,384,64]{1,2,0:T(8,128)(2,1)} %get-tuple-element.542, s32[]{:T(128)S(6)} %select_n.48), kind=kOutput, calls=%fused_computation.3.clone.1 | convolution fusion | flops 77263872 | bytes 3125252 | tf_op jit(solution)/shard_map/while/body/dot_general | solution.py:59
  27.3 0.5 select_reduce_fusion.5
  27.8 8.3 %all_gather.11 = bf16[384,128]{1,0:T(8,128)(2,1)S(1)} all-gather(bf16[192,128]{1,0:T(8,128)(2,1)S(1)} %copy-done.9), channel_id=1, replica_groups=mesh['dp'=4,'ctx'=2,'tp'=4] {'ctx'}, dimensions={0}, use_global_device_ids=true | all-gather | bytes 147456 | tf_op jit(solution)/shard_map/all_gather | solution.py:47
  36.1 0.8 copy.32
  36.9 0.6 log_add_fusion
  37.6 3.4 %while.37 = (s32[]{:T(128)}, f32[2,1536,64]{1,2,0:T(8,128)S(1)}, s32[]{:T(128)}, s32[]{:T(128)}, s32[384]{0:T(512)S(1)}, /*index=5*/s32[192]{0:T(256)S(1)}, bf16...) while((s32[]{:T(128)}, f32[2,1536,64]{1,2,0:T(8,128)S(1)}, ...), condition=%wide.region_5.6_spmd, body=%wide.region_4.5_spmd.sunk | while | flops 153661824 | bytes 3370175 | solution.py:105
  37.6 0.1 dynamic_slice.62
  37.7 0.1 compare_and_fusion.7
  37.8 0.2 tile.35
  38.0 0.7 tile.36
  38.7 2.2 %convolution_add_fusion.2 = f32[2,1536,64]{1,2,0:T(8,128)S(1)} fusion(f32[2,1536,64]{1,2,0:T(8,128)S(1)} %get-tuple-element.563, bf16[2,1536,64]{1,2,0:T(8,128)(2,1)} %get-tuple-element.583, f32[2,1536]{1,0:T(2,128)} %get-tuple-element.584, pred[1536,192]{0,1:T(8,128)(4,1)S(1)} %tile.36, bf16[2,384,64]{1,2,0:T(8,128)(2,1)} %get-tuple-element.585, ...), kind=kOutput, calls=%fused_computation.16.clone.1 | convolution fusion | flops 153550848 | bytes 2405376 | tf_op jit(solution)/shard_map/while/body/dot_general | solution.py:101
  41.0 0.2 copy.33
  41.2 0.3 copy.34
  41.5 1.2 reshape.254
  42.6 1.1 multiply_reduce_fusion
  43.8 1.0 broadcast.187
  44.7 0.7 broadcast.188.clone
  45.4 0.7 broadcast.188.clone2
  46.1 19.8 %while.38 = (s32[]{:T(128)}, f32[2,1536,64]{1,2,0:T(8,128)}, f32[384,128]{1,0:T(8,128)}, f32[384,128]{1,0:T(8,128)}, s32[]{:T(128)}, /*index=5*/s32[]{:T(128)}, ...) while((s32[]{:T(128)}, f32[2,1536,64]{1,2,0:T(8,128)}, ...), condition=%wide.region_8.9_spmd, body=%wide.region_7.8_spmd.sunk | while | flops 382194048 | bytes 19188072 | solution.py:150
  46.2 0.1 compare_and_fusion.8
  46.3 0.2 tile.37
  46.5 0.7 tile.38
  47.3 1.9 %fusion.75 = f32[2,1536,192]{1,2,0:T(8,128)S(1)} fusion(bf16[2,1536,64]{1,2,0:T(8,128)(2,1)} %get-tuple-element.635, f32[2,1536]{1,0:T(2,128)} %get-tuple-element.636, pred[1536,192]{0,1:T(8,128)(4,1)S(1)} %tile.38, bf16[2,384,64]{1,2,0:T(8,128)(2,1)} %get-tuple-element.634, s32[]{:T(128)S(6)} %select_n.52), kind=kOutput, calls=%fused_computation.34.clone.1 | convolution fusion | flops 77266944 | bytes 3125252 | tf_op jit(solution)/shard_map/while/body/dot_general | solution.py:59
  49.2 1.7 %fusion.76 = bf16[2,1536,192]{1,2,0:T(8,128)(2,1)S(1)} fusion(f32[2,1536,192]{1,2,0:T(8,128)S(1)} %fusion.75, bf16[2,1536,64]{1,2,0:T(8,128)(2,1)} %get-tuple-element.638, f32[2,1536]{1,0:T(2,128)S(1)} %get-tuple-element.639, bf16[2,384,64]{1,2,0:T(8,128)(2,1)} %get-tuple-element.637, s32[]{:T(128)S(6)} %select_n.52), kind=kOutput, calls=%fused_computation.37.clone.1 | convolution fusion | flops 77266944 | bytes 4009988 | tf_op jit(solution)/shard_map/while/body/dot_general | solution.py:125
  50.8 2.1 %convolution_multiply_fusion.6 = f32[2,192,64]{1,2,0:T(8,128)} fusion(bf16[2,1536,192]{1,2,0:T(8,128)(2,1)S(1)} %fusion.76, bf16[2,1536,64]{1,2,0:T(8,128)(2,1)} %get-tuple-element.635), kind=kOutput, calls=%fused_computation.42.clone.1 | convolution fusion | flops 75522048 | bytes 1671168 | tf_op jit(solution)/shard_map/while/body/dot_general | solution.py:137
  53.0 0.6 constant_dynamic-slice_fusion.5
  53.6 1.7 %copy.53 = f32[192,128]{0,1:T(8,128)} copy(f32[192,128]{1,0:T(8,128)} %constant_dynamic-slice_fusion.5) | data formatting | bytes 196608 | tf_op jit(solution)/shard_map/while/body/dynamic_slice | solution.py:35
  55.3 1.6 %bitcast_add_fusion.5 = f32[192,128]{0,1:T(8,128)} fusion(f32[192,128]{0,1:T(8,128)} %copy.53, f32[2,192,64]{1,2,0:T(8,128)} %convolution_multiply_fusion.6), kind=kLoop, calls=%fused_computation.45.clone.1 | loop fusion | flops 24576 | bytes 294912 | tf_op jit(solution)/shard_map/while/body/add | solution.py:36
  56.9 1.6 %copy.54 = f32[192,128]{1,0:T(8,128)} copy(f32[192,128]{0,1:T(8,128)} %bitcast_add_fusion.5) | data formatting | bytes 196608 | tf_op jit(solution)/shard_map/while/body/dynamic_update_slice | solution.py:36
  58.6 2.2 %fusion.78 = f32[2,192,64]{1,2,0:T(8,128)} fusion(bf16[2,1536,64]{1,2,0:T(8,128)(2,1)} %get-tuple-element.638, f32[2,1536,192]{1,2,0:T(8,128)S(1)} %fusion.75), kind=kOutput, calls=%fused_computation.40.clone.1 | convolution fusion | flops 76087296 | bytes 2850816 | tf_op jit(solution)/shard_map/while/body/dot_general | solution.py:142
  60.8 0.1 copy.51
  60.9 0.9 bitcast_add_fusion.4
  61.8 0.1 copy.52
  61.9 1.6 %constant_dynamic-update-slice_fusion.3 = (f32[384,128]{1,0:T(8,128)}, f32[384,128]{1,0:T(8,128)}) fusion(f32[384,128]{1,0:T(8,128)} %get-tuple-element.611, f32[192,128]{1,0:T(8,128)S(1)} %copy.52, s32[]{:T(128)S(6)} %select_n.52, f32[384,128]{1,0:T(8,128)} %get-tuple-element.610, f32[192,128]{1,0:T(8,128)} %copy.54), kind=kLoop, calls=%fused_computation.50.clone.1 | loop fusion | bytes 393220 | tf_op jit(solution)/shard_map/while/body/dynamic_update_slice | solution.py:36
  63.5 2.5 %fusion.77 = f32[2,1536,64]{1,2,0:T(8,128)} fusion(f32[2,1536,64]{1,2,0:T(8,128)} %get-tuple-element.609, bf16[2,1536,192]{1,2,0:T(8,128)(2,1)S(1)} %fusion.76, bf16[2,384,64]{1,2,0:T(8,128)(2,1)} %get-tuple-element.634, s32[]{:T(128)S(6)} %select_n.52), kind=kOutput, calls=%fused_computation.39.clone.1 | convolution fusion | flops 75890688 | bytes 2818052 | tf_op jit(solution)/shard_map/while/body/dot_general | solution.py:131
  66.0 0.7 reduce-scatter.5.cloned.1.call-update
  66.7 1.2 convert_element_type.31
  67.9 0.4 convert_element_type.32
  68.3 0.1 copy.35
  68.4 0.9 copy.38
  69.4 0.7 exponential_multiply_fusion
  70.1 0.1 reshape.255
  70.2 0.1 reduce_sum.28
  70.3 0.1 neg.7
  70.4 28.5 %psum.7 = f32[16]{0:T(128)} all-reduce(f32[16]{0:T(128)S(1)} %neg.7), channel_id=1, replica_groups=mesh['dp'=4,'ctx'=2,'tp'=4] {'ctx'}, use_global_device_ids=true, to_apply=%region_12.13 | all-reduce | flops 16 | bytes 128 | tf_op jit(solution)/shard_map/psum | solution.py:111
  98.9 3.1 %reduce-scatter.3.cloned.1.call-done = f32[192,128]{1,0:T(8,128)} async-done(((f32[384,128]{1,0:T(8,128)}), f32[192,128]{1,0:T(8,128)}) %reduce-scatter.3.cloned.1.call-update) | async-done | bytes 98320 | tf_op jit(solution)/shard_map/reduce_scatter | solution.py:155
  102.1 1.5 %convert_element_type.35 = bf16[192,128]{1,0:T(8,128)(2,1)} convert(f32[192,128]{1,0:T(8,128)} %reduce-scatter.3.cloned.1.call-done) | non-fusion elementwise | flops 24576 | bytes 147456 | tf_op jit(solution)/shard_map/convert_element_type | solution.py:160
  103.6 11.8 %reduce-scatter.5.cloned.1.call-done = f32[192,128]{1,0:T(8,128)} async-done(((f32[384,128]{1,0:T(8,128)}), f32[192,128]{1,0:T(8,128)}) %reduce-scatter.5.cloned.1.call-update) | async-done | bytes 98320 | tf_op jit(solution)/shard_map/reduce_scatter | solution.py:156
  115.4 1.5 %convert_element_type.36 = bf16[192,128]{1,0:T(8,128)(2,1)} convert(f32[192,128]{1,0:T(8,128)} %reduce-scatter.5.cloned.1.call-done) | non-fusion elementwise | flops 24576 | bytes 147456 | tf_op jit(solution)/shard_map/convert_element_type | solution.py:161
  (40 shorter events, 0.5 us)
Async XLA Ops:
  7.2 16.6 %copy-start.3 = (s32[192]{0:T(256)S(1)}, s32[192]{0:T(256)}, u32[]{:S(2)}) copy-start(s32[192]{0:T(256)} %param.16) | copy-start | bytes 2308
  7.2 10.8 %copy-start.8 = (bf16[192,128]{1,0:T(8,128)(2,1)S(1)}, bf16[192,128]{1,0:T(8,128)(2,1)}, u32[]{:S(2)}) copy-start(bf16[192,128]{1,0:T(8,128)(2,1)} %param.13) | copy-start | bytes 147460
  7.2 16.3 %copy-start.10 = (f32[16]{0:T(128)S(1)}, f32[16]{0:T(128)}, u32[]{:S(2)}) copy-start(f32[16]{0:T(128)} %param.17) | copy-start | bytes 196
  7.2 94.9 %reduce-scatter.3.cloned.1.call-start = ((), (), s32[]{:S(2)}) async-start(), calls=%async_computation.2 | async-start | bytes 294912 | tf_op jit(solution)/shard_map/reduce_scatter | solution.py:155
  23.7 0.6 copy-start.6
  23.7 4.1 %copy-start.9 = (bf16[192,128]{1,0:T(8,128)(2,1)S(1)}, bf16[192,128]{1,0:T(8,128)(2,1)}, u32[]{:S(2)}) copy-start(bf16[192,128]{1,0:T(8,128)(2,1)} %param.14) | copy-start | bytes 147460
  37.6 3.4 %copy-start.2 = (bf16[192,1024]{1,0:T(8,128)(2,1)S(1)}, bf16[192,1024]{1,0:T(8,128)(2,1)}, u32[]{:S(2)}) copy-start(bf16[192,1024]{1,0:T(8,128)(2,1)} %param.15) | copy-start | bytes 1179652
  46.1 1.2 copy-start.4
  49.2 3.8 %copy-start = (f32[384,128]{1,0:T(8,128)S(1)}, f32[384,128]{1,0:T(8,128)}, u32[]{:S(2)}) copy-start(f32[384,128]{1,0:T(8,128)} %get-tuple-element.610) | copy-start | bytes 589828 | tf_op jit(solution)/shard_map/while
  58.6 2.2 %copy-start.1 = (f32[384,128]{1,0:T(8,128)S(1)}, f32[384,128]{1,0:T(8,128)}, u32[]{:S(2)}) copy-start(f32[384,128]{1,0:T(8,128)} %get-tuple-element.611) | copy-start | bytes 589828 | tf_op jit(solution)/shard_map/while
  60.7 5.2 %copy-start.5 = (s32[384]{0:T(512)S(1)}, s32[384]{0:T(512)}, u32[]{:S(2)}) copy-start(s32[384]{0:T(512)} %copy-done.4) | copy-start | bytes 4612 | tf_op jit(solution)/shard_map/while
  65.9 3.4 %copy-start.7 = (f32[2,1536]{1,0:T(2,128)S(1)}, f32[2,1536]{1,0:T(2,128)}, u32[]{:S(2)}) copy-start(f32[2,1536]{1,0:T(2,128)} %copy-done.6) | copy-start | bytes 36868
  66.0 49.4 %reduce-scatter.5.cloned.1.call-start = ((), (), s32[]{:S(2)}) async-start(), calls=%async_computation.3 | async-start | bytes 294912 | tf_op jit(solution)/shard_map/reduce_scatter | solution.py:156
Sparse Core Ops, SparseCore 0:
  66.1 35.9 reduce-scatter.2
  104.3 11.0 reduce-scatter.4
where the time goes:
time: 125 us; the launch traced here: 124 us
  blocking collectives  46.8 us (37%)
  local copies, waits for them, and re-layouts  21.6 us (17%)
  waiting for transfers between devices  15.7 us (13%)
  between operations  14.9 us (12%)
  matrix products  14.3 us (11%)
  other arithmetic  10.2 us (8%)
    psum x1, blocking collectives, on_device(): grad_sinks = lax.psum(sink_term, 'ctx')  28.5 us
    reduce_scatter x1, waiting for transfers between devices, on_device(): lax.psum_scatter(value_buf, 'ctx', scatter_dimension=0, tiled=True)  11.8 us
    all_gather x1, blocking collectives, on_device(): lax.all_gather(values, 'ctx', axis=0, tiled=True)  8.27 us
    unnamed x1, blocking collectives  5.25 us
    unnamed x21, local copies, waits for them, and re-layouts  5.05 us
    all_gather x1, blocking collectives, on_device(): lax.all_gather(keys, 'ctx', axis=0, tiled=True)  4.75 us
    dot_general x2, matrix products, tile_scores(): lax.dot_general(query_heads, key_block, (((2,), (2,)), ((0,), (0,))), pre...  3.68 us
    dynamic_update_slice x3, local copies, waits for them, and re-layouts, add_rows(): return lax.dynamic_update_slice_in_dim(buffer, before + flat, start, 0)  3.32 us
  transfers between devices with their start and end apart: 2, of which 2 were waited for; matrix products, arithmetic and copies ran while one was open for 4% of the time, Pallas kernels for 0%

commit v1 on v0

v1 whole, which is shorter than its diff:
```python
import functools

import jax
import jax.numpy as jnp
from jax import lax
from jax.experimental import pallas as pl
from jax.experimental.pallas import tpu as pltpu
from jax.sharding import PartitionSpec as P

HEAD_SIZE = 64
LANES = 128
BLOCK = 64
NEG = -1e30
F32 = jnp.float32
BF16 = jnp.bfloat16


def dot(left, right, left_dim, right_dim):
    return lax.dot_general(
        left, right, (((left_dim,), (right_dim,)), ((), ())), preferred_element_type=F32
    )


def over_tiles(count, body, carry):
    if count == 1:
        return body(0, carry)
    return lax.fori_loop(0, count, body, carry)


class Keep:
    def __init__(self, ref, count):
        self.ref, self.inline = ref, count == 1

    def put(self, tile, value):
        if self.inline:
            self.value = value
        else:
            self.ref[tile] = value

    def get(self, tile):
        return self.value if self.inline else self.ref[tile]


def columns(row):
    return jnp.broadcast_to(row, (LANES, row.shape[1])).T


def split_halves(block):
    lane = lax.broadcasted_iota(jnp.int32, block.shape, 1)
    wide = block.astype(F32)
    turned = pltpu.roll(wide, HEAD_SIZE, 1)
    low = lane < HEAD_SIZE
    zero = jnp.zeros_like(wide)
    first = (jnp.where(low, wide, zero), jnp.where(low, zero, turned))
    second = (jnp.where(low, turned, zero), jnp.where(low, zero, wide))
    return tuple((a.astype(BF16), b.astype(BF16)) for a, b in (first, second))


def seg_features(seg_col, blocked):
    lane = lax.broadcasted_iota(jnp.int32, seg_col.shape, 1)
    other = (lane - BLOCK) != seg_col.astype(jnp.int32)
    if blocked is not None:
        other = other | blocked
    return jnp.where((lane >= BLOCK) & other, NEG, 0.0)


def merge_heads(parts):
    lane = lax.broadcasted_iota(jnp.int32, parts[0][0].shape, 1)
    low = lane < HEAD_SIZE
    (first_low, first_high), (second_low, second_high) = parts
    straight = jnp.where(low, first_low, second_high)
    crossed = jnp.where(low, second_low, first_high)
    return straight + pltpu.roll(crossed, HEAD_SIZE, 1)


def main_kernel(
    remote, ctx_axis, kv_heads, pairs,
    q_ref, k_ref, v_ref, g_ref, seg_ref, sink_ref, far_ref,
    dq_ref, own_ref, part_ref, sinks_out_ref,
    s_keep, dp_keep, p_keep, ds_keep, lhs_keep,
):
    length = q_ref.shape[0]
    blocks = length // BLOCK
    width = pairs * BLOCK
    scale = HEAD_SIZE ** (-0.5)
    place = lax.axis_index(ctx_axis)

    seg_col = columns(seg_ref[...].astype(F32))
    lane = lax.broadcasted_iota(jnp.int32, (length, LANES), 1)
    row = lax.broadcasted_iota(jnp.int32, (length, LANES), 0)
    inner = row % BLOCK
    key_seg = seg_features(seg_col, None)
    key_plain = key_seg.astype(BF16)
    key_diag = jnp.where(lane == inner, 1.0, key_seg).astype(BF16)
    same = (lane - BLOCK) == seg_col.astype(jnp.int32)
    query_feat = jnp.where(
        lane < BLOCK, jnp.where(lane > inner, NEG, 0.0), jnp.where(same, 1.0, 0.0)
    ).astype(BF16)

    lane_row = lax.broadcasted_iota(jnp.int32, (1, width), 1)
    far_feat = Keep(lhs_keep, remote)

    def make_feat(tile, carry):
        far = far_ref[tile]
        rows = far[2 * length :].astype(F32)
        pieces = [columns(rows[i : i + 1]) for i in range(-(-length // LANES))]
        far_col = jnp.concatenate(pieces, axis=0)[:length]
        gone = jnp.full((length, LANES), place - 1 - tile) < 0
        far_feat.put(tile, seg_features(far_col, gone).astype(BF16))
        return carry

    over_tiles(remote, make_feat, 0)

    for first in range(0, kv_heads, 2):
        span = slice(first * HEAD_SIZE, (first + 2) * HEAD_SIZE)
        key_halves = split_halves(k_ref[:, span].astype(F32) * scale)
        value_halves = split_halves(v_ref[:, span])
        key_sums, value_sums, far_key_sums, far_value_sums = [], [], {}, {}
        for local in range(2):
            head = first + local
            keys, values = key_halves[local], value_halves[local]
            p_diag, ds_diag, q_rows, g_rows = [], [], [], []
            far_p = [Keep(p_keep.at[block], remote) for block in range(blocks)]
            far_ds = [Keep(ds_keep.at[block], remote) for block in range(blocks)]

            def far_halves(tile, which, local=local, span=span):
                start = which * length
                block = far_ref[tile, start : start + length, span]
                factor = scale if which == 0 else 1.0
                return split_halves(block.astype(F32) * factor)[local]

            sink_rows = [None, None]
            sink_sums = [0.0, 0.0]
            for half in range(2):
                sink_row = jnp.zeros((1, width), F32)
                for pair in range(pairs):
                    value = sink_ref[head * 2 * pairs + 2 * pair + half]
                    sink_row = jnp.where(lane_row // BLOCK == pair, value, sink_row)
                sink_rows[half] = sink_row

            for block in range(blocks):
                rows = slice(block * BLOCK, (block + 1) * BLOCK)
                count = (block + 1) * BLOCK
                lanes_of = [
                    slice((head * pairs + pair) * LANES, (head * pairs + pair + 1) * LANES)
                    for pair in range(pairs)
                ]
                q_stack = jnp.concatenate([q_ref[rows, at] for at in lanes_of], axis=0)
                g_stack = jnp.concatenate([g_ref[rows, at] for at in lanes_of], axis=0)
                feat = jnp.concatenate([query_feat[rows]] * pairs, axis=0)
                q_wide = jnp.concatenate([q_stack, feat], axis=1)
                q_rows.append(q_stack)
                g_rows.append(g_stack)

                feat_k = key_diag[rows]
                if block:
                    feat_k = jnp.concatenate([key_plain[: count - BLOCK], feat_k], axis=0)
                key_near = jnp.concatenate([keys[0][:count], keys[1][:count]], axis=0)
                key_wide = jnp.concatenate(
                    [key_near, jnp.concatenate([feat_k, feat_k], axis=0)], axis=1
                )
                value_near = jnp.concatenate([values[0][:count], values[1][:count]], axis=0)

                s_near = dot(key_wide, q_wide, 1, 1)
                tops = [
                    jnp.maximum(
                        jnp.max(s_near[half * count : (half + 1) * count], axis=0, keepdims=True),
                        sink_rows[half],
                    )
                    for half in range(2)
                ]
                far_s, far_dp = Keep(s_keep, remote), Keep(dp_keep, remote)

                def halves(array):
                    return array[:length], array[length:]

                def spread(pair_of_rows, size):
                    return jnp.concatenate(
                        [jnp.broadcast_to(r, (size, width)) for r in pair_of_rows], axis=0
                    )

                def score_far(tile, carry):
                    low, high = far_halves(tile, 0)
                    feats = far_feat.get(tile)
                    wide = jnp.concatenate(
                        [
                            jnp.concatenate([low, high], axis=0),
                            jnp.concatenate([feats, feats], axis=0),
                        ],
                        axis=1,
                    )
                    scores = dot(wide, q_wide, 1, 1)
                    far_s.put(tile, scores)
                    return tuple(
                        jnp.maximum(c, jnp.max(part, axis=0, keepdims=True))
                        for c, part in zip(carry, halves(scores))
                    )

                tops = over_tiles(remote, score_far, tuple(tops))
                e_near = jnp.exp(s_near - spread(tops, count))
                sink_mass = [jnp.exp(sink_rows[half] - tops[half]) for half in range(2)]
                mass = tuple(
                    sink_mass[half]
                    + jnp.sum(e_near[half * count : (half + 1) * count], axis=0, keepdims=True)
                    for half in range(2)
                )

                def mass_far(tile, carry):
                    weight = jnp.exp(far_s.get(tile) - spread(tops, length))
                    far_s.put(tile, weight)
                    return tuple(
                        c + jnp.sum(part, axis=0, keepdims=True)
                        for c, part in zip(carry, halves(weight))
                    )

                mass = over_tiles(remote, mass_far, mass)
                inverse = [1.0 / m for m in mass]
                p_near = e_near * spread(inverse, count)
                p_half = p_near.astype(BF16)
                p_diag.append(p_half)
                dp_near = dot(value_near, g_stack, 1, 1)
                prod = p_half.astype(F32) * dp_near
                delta = tuple(
                    jnp.sum(prod[half * count : (half + 1) * count], axis=0, keepdims=True)
                    for half in range(2)
                )

                def delta_far(tile, carry):
                    prob = far_s.get(tile) * spread(inverse, length)
                    far_s.put(tile, prob)
                    rounded = prob.astype(BF16)
                    far_p[block].put(tile, rounded)
                    low, high = far_halves(tile, 1)
                    dprob = dot(jnp.concatenate([low, high], axis=0), g_stack, 1, 1)
                    far_dp.put(tile, dprob)
                    return tuple(
                        c + jnp.sum(part, axis=0, keepdims=True)
                        for c, part in zip(carry, halves(rounded.astype(F32) * dprob))
                    )

                delta = over_tiles(remote, delta_far, delta)
                for half in range(2):
                    sink_sums[half] = (
                        sink_sums[half] - sink_mass[half] * inverse[half] * delta[half]
                    )
                ds_near = (p_near * (dp_near - spread(delta, count))).astype(BF16)
                ds_diag.append(ds_near)
                dq = dot(ds_near, key_near, 0, 0)

                def dscore_far(tile, carry):
                    dscore = far_s.get(tile) * (far_dp.get(tile) - spread(delta, length))
                    dscore = dscore.astype(BF16)
                    far_ds[block].put(tile, dscore)
                    low, high = far_halves(tile, 0)
                    return carry + dot(dscore, jnp.concatenate([low, high], axis=0), 0, 0)

                dq = over_tiles(remote, dscore_far, dq)
                for pair in range(pairs):
                    dq_ref[rows, lanes_of[pair]] = dq[pair * BLOCK : (pair + 1) * BLOCK].astype(
                        BF16
                    )

            for half in range(2):
                sinks_out_ref[2 * head + half : 2 * head + half + 1, :] = sink_sums[half]

            def near_sum(parts, rows_of):
                out = [[], []]
                for kb in range(blocks):
                    left = []
                    for block in range(kb, blocks):
                        count = (block + 1) * BLOCK
                        low = parts[block][kb * BLOCK : (kb + 1) * BLOCK]
                        high = parts[block][count + kb * BLOCK : count + (kb + 1) * BLOCK]
                        left.append(jnp.concatenate([low, high], axis=0))
                    total = dot(
                        jnp.concatenate(left, axis=1), jnp.concatenate(rows_of[kb:], axis=0), 1, 0
                    )
                    out[0].append(total[:BLOCK])
                    out[1].append(total[BLOCK:])
                return tuple(jnp.concatenate(o, axis=0) for o in out)

            value_sums.append(near_sum(p_diag, g_rows))
            key_sums.append(near_sum(ds_diag, q_rows))
            q_all = jnp.concatenate(q_rows, axis=0)
            g_all = jnp.concatenate(g_rows, axis=0)

            def far_sum(tile, carry, local=local):
                for which, parts, right in ((0, far_ds, q_all), (1, far_p, g_all)):
                    left = jnp.concatenate([part.get(tile) for part in parts], axis=1)
                    total = dot(left, right, 1, 0)
                    if remote == 1:
                        (far_key_sums, far_value_sums)[which][local] = halves(total)
                    else:
                        at = slice(which * length, (which + 1) * length)
                        lane = lax.broadcasted_iota(jnp.int32, (length, LANES), 1)
                        low = lane < HEAD_SIZE
                        a, b = halves(total)
                        turned = pltpu.roll(jnp.where(low, a, b), HEAD_SIZE, 1)
                        both = (a if local == 0 else b) + turned
                        keep = low if local == 0 else ~low
                        factor = scale if which == 0 else 1.0
                        old = part_ref[tile, at, span]
                        part_ref[tile, at, span] = jnp.where(
                            keep, (both * factor).astype(BF16), old
                        )
                return carry

            over_tiles(remote, far_sum, 0)

        own_ref[0, :, span] = merge_heads(key_sums) * scale
        own_ref[1, :, span] = merge_heads(value_sums)
        if remote == 1:
            part_ref[0, :length, span] = (merge_heads([far_key_sums[i] for i in range(2)]) * scale).astype(BF16)
            part_ref[0, length : 2 * length, span] = merge_heads(
                [far_value_sums[i] for i in range(2)]
            ).astype(BF16)

    sink_rest = sinks_out_ref[...]
    thirds = []
    for _ in range(3):
        top = sink_rest.astype(BF16)
        thirds.append(top)
        sink_rest = sink_rest - top.astype(F32)
    for tile in range(remote):
        for i, piece in enumerate(thirds):
            for j in range(width // LANES):
                at = 2 * length + 16 * (i * (width // LANES) + j)
                part_ref[tile, at : at + 2 * kv_heads, 0:LANES] = piece[:, j * LANES : (j + 1) * LANES]


def last_kernel(remote, pairs, own_ref, back_ref, sinks_ref, dk_ref, dv_ref, out_ref):
    length = dk_ref.shape[0]
    totals = [own_ref[0], own_ref[1]]
    sink = sinks_ref[...]
    heads2 = sink.shape[0]
    width = sink.shape[1]
    for tile in range(remote):
        for which in range(2):
            at = slice(which * length, (which + 1) * length)
            totals[which] = totals[which] + back_ref[tile, at].astype(F32)
        rest = jnp.zeros_like(sink)
        for i in range(3):
            pieces = []
            for j in range(width // LANES):
                at = 2 * length + 16 * (i * (width // LANES) + j)
                pieces.append(back_ref[tile, at : at + heads2, 0:LANES].astype(F32))
            rest = rest + jnp.concatenate(pieces, axis=1)
        sink = sink + rest
    dk_ref[...] = totals[0].astype(BF16)
    dv_ref[...] = totals[1].astype(BF16)
    lane = lax.broadcasted_iota(jnp.int32, (heads2, width), 1)
    out_lane = lax.broadcasted_iota(jnp.int32, out_ref.shape, 1)
    line = jnp.zeros(out_ref.shape, F32)
    for pair in range(pairs):
        sums = jnp.sum(jnp.where(lane // BLOCK == pair, sink, 0.0), axis=1, keepdims=True)
        for r in range(heads2):
            at = (r // 2) * 2 * pairs + 2 * pair + r % 2
            line = jnp.where(out_lane == at, sums[r : r + 1], line)
    out_ref[...] = line


def on_device(ctx_size, queries, keys, values, grad_out, segments, sinks):
    length = queries.shape[0]
    kv_heads = keys.shape[1] // HEAD_SIZE
    pairs = queries.shape[1] // keys.shape[1] // 2
    width = pairs * BLOCK
    blocks = length // BLOCK
    remote = ctx_size - 1
    cols = keys.shape[1]

    seg_rows = -(-length // LANES)
    seg_line = jnp.pad(segments, (0, seg_rows * LANES - length)).astype(BF16)
    seg_block = jnp.pad(
        seg_line.reshape(seg_rows, LANES), ((0, 16 - seg_rows), (0, cols - LANES))
    )
    packed = jnp.concatenate([keys, values, seg_block], axis=0)

    def turn(array, shift):
        order = [(i, (i + shift) % ctx_size) for i in range(ctx_size)]
        return lax.ppermute(array, "ctx", order)

    far = jnp.stack([turn(packed, s) for s in range(1, ctx_size)])

    extra = 16 * 3 * (width // LANES)
    tall = 2 * length + extra
    vmem = pl.BlockSpec(memory_space=pltpu.VMEM)
    smem = pl.BlockSpec(memory_space=pltpu.SMEM)
    many = remote if remote > 1 else 1
    small = remote == 1

    def scratch(shape, dtype):
        return pltpu.VMEM((8, LANES) if small else shape, dtype)

    dq, own, part, sink_rows = pl.pallas_call(
        functools.partial(main_kernel, remote, "ctx", kv_heads, pairs),
        out_shape=(
            jax.ShapeDtypeStruct(queries.shape, BF16),
            jax.ShapeDtypeStruct((2,) + keys.shape, F32),
            jax.ShapeDtypeStruct((remote, tall, cols), BF16),
            jax.ShapeDtypeStruct((2 * kv_heads, width), F32),
        ),
        in_specs=[vmem, vmem, vmem, vmem, vmem, smem, vmem],
        out_specs=(vmem, vmem, vmem, vmem),
        scratch_shapes=[
            pltpu.VMEM((1, 8, LANES) if small else (many, 2 * length, width), F32),
            pltpu.VMEM((1, 8, LANES) if small else (many, 2 * length, width), F32),
            pltpu.VMEM((blocks, 1, 16, LANES) if small else (blocks, many, 2 * length, width), BF16),
            pltpu.VMEM((blocks, 1, 16, LANES) if small else (blocks, many, 2 * length, width), BF16),
            pltpu.VMEM((1, 16, LANES) if small else (many, length, LANES), BF16),
        ],
    )(queries, keys, values, grad_out, segments.reshape(1, length), sinks, far)

    back = jnp.stack([turn(part[s - 1], -s) for s in range(1, ctx_size)])
    heads = sinks.shape[0]
    dk, dv, line = pl.pallas_call(
        functools.partial(last_kernel, remote, pairs),
        out_shape=(
            jax.ShapeDtypeStruct(keys.shape, BF16),
            jax.ShapeDtypeStruct(values.shape, BF16),
            jax.ShapeDtypeStruct((1, heads), F32),
        ),
        in_specs=[vmem, vmem, vmem],
        out_specs=(vmem, vmem, vmem),
    )(own, back, sink_rows)
    return dq, dk, dv, line.reshape(heads)


def solution(mesh):
    rows = P(("dp", "ctx"), "tp")
    return jax.shard_map(
        functools.partial(on_device, mesh.shape["ctx"]),
        mesh=mesh,
        in_specs=(rows, rows, rows, rows, P(("dp", "ctx")), P("tp")),
        out_specs=(rows, rows, rows, P(("dp", "tp"))),
        check_vma=False,
    )
```

time: 125 us -> 23.4 us (0.19)
  blocking collectives: 46.8 us -> 0 us
  local copies, waits for them, and re-layouts: 21.6 us -> 1.29 us
  matrix products: 14.3 us -> 0 us
  between operations: 14.9 us -> 0.64 us
  waiting for transfers between devices: 15.7 us -> 6.19 us
  Pallas kernels: 0 us -> 8.68 us
  other arithmetic: 10.2 us -> 1.52 us
  starting transfers between devices: 0.08 us -> 4.83 us
    psum x1 -> x0, blocking collectives: 28.5 us -> none  [on_device(): grad_sinks = lax.psum(sink_term, 'ctx')]
    reduce_scatter x2 -> x0, waiting for transfers between devices: 15 us -> none  [the longest x1 11.8 us: on_device(): lax.psum_scatter(value_buf, 'ctx', scatter_dimension=0, tiled=True)]
    dot_general x7 -> x0, matrix products: 14.3 us -> none  [the longest x2 3.68 us: tile_scores(): lax.dot_general(query_heads, key_block, (((2,), (2,)), ((0,), (0,))), pre...]
    all_gather x2 -> x0, blocking collectives: 13 us -> none  [the longest x1 8.27 us: on_device(): lax.all_gather(values, 'ctx', axis=0, tiled=True)]
    pallas_call x0 -> x2, Pallas kernels: none -> 8.68 us  [the longest x1 7.04 us: on_device(): pl.pallas_call(functools.partial(main_kernel, remote, 'ctx', kv_heads, pa...]
    ppermute x0 -> x2, waiting for transfers between devices: none -> 6.19 us  [turn(): return lax.ppermute(array, 'ctx', order)]
    unnamed x1 -> x0, blocking collectives: 5.25 us -> none
    another operation x10 -> x0, local copies, waits for them, and re-layouts: 5.22 us -> none  [the longest x6 2.78 us: tile_scores(): allowed = jnp.tile(allowed, (query_group, 1))[None]]
  transfers between devices with their start and end apart: 2 -> 2, of which waited for: 2 -> 2; matrix products, arithmetic and copies ran while one was open for 4% -> 0% of each run, Pallas kernels for 0% -> 0%
where the time goes in v1:
time: 23.4 us; the launch traced here: 23.1 us
  Pallas kernels  8.68 us (37%)
  waiting for transfers between devices  6.19 us (26%)
  starting transfers between devices  4.83 us (21%)
  other arithmetic  1.52 us (6%)
  local copies, waits for them, and re-layouts  1.29 us (6%)
  between operations  0.64 us (3%)
    pallas_call x1, Pallas kernels, on_device(): pl.pallas_call(functools.partial(main_kernel, remote, 'ctx', kv_heads, pa...  7.04 us
    ppermute x2, waiting for transfers between devices, turn(): return lax.ppermute(array, 'ctx', order)  6.19 us
    ppermute x2, starting transfers between devices, turn(): return lax.ppermute(array, 'ctx', order)  4.83 us
    pallas_call x1, Pallas kernels, on_device(): pl.pallas_call(functools.partial(last_kernel, remote, pairs), out_shape=(...  1.64 us
    unnamed x4, local copies, waits for them, and re-layouts  1.28 us
    concatenate x1, other arithmetic, on_device(): packed = jnp.concatenate([keys, values, seg_block], axis=0)  0.83 us
    another operation x1, other arithmetic  0.68 us
  transfers between devices with their start and end apart: 2, of which 2 were waited for; matrix products, arithmetic and copies ran while one was open for 0% of the time, Pallas kernels for 0%

profile of v1, /device:TPU:0, one launch (start us, length us, event | category | flops | bytes accessed | tf_op | source)
XLA Modules:
  0.0 23.1 jit_solution(225509853070930084)
XLA Ops:
  0.6 0.7 %convert.4 = bf16[192]{0:T(256)(128)(2,1)S(1)} convert(s32[192]{0:T(256)} %param.10) | non-fusion elementwise | flops 192 | bytes 1152 | tf_op jit(solution)/shard_map/convert
  1.3 0.8 %fusion.1 = bf16[400,128]{1,0:T(8,128)(2,1)S(1)} fusion(bf16[2,128]{1,0:T(2,128)(2,1)S(1)} %pad_bitcast_fusion, bf16[192,128]{1,0:T(8,128)(2,1)} %v_ref.1, bf16[192,128]{1,0:T(8,128)(2,1)} %k_ref.1), kind=kLoop, calls=%fused_computation.2 | loop fusion | flops 409600 | bytes 201216 | tf_op jit(solution)/shard_map/concatenate | solution.py:376
  2.2 3.0 %collective-permute-start = (bf16[400,128]{1,0:T(8,128)(2,1)S(1)}, bf16[400,128]{1,0:T(8,128)(2,1)S(1)}, u32[]{:S(2)}, u32[]{:S(2)}) collective-permute-start(bf16[400,128]{1,0:T(8,128)(2,1)S(1)} %fusion.1), channel_id=1, source_target_pairs={{0,4},{4,0},{1,5},{5,1},{2,6},{6,2},{3,7},{7,3},{8,12},{12,8},{9,1... | collective-permute-start | bytes 307208 | tf_op jit(solution)/shard_map/ppermute | solution.py:380
  5.2 2.9 %collective-permute-done = bf16[400,128]{1,0:T(8,128)(2,1)S(1)} collective-permute-done((bf16[400,128]{1,0:T(8,128)(2,1)S(1)}, bf16[400,128]{1,0:T(8,128)(2,1)S(1)}, u32[]{:S(2)}, u32[]{:S(2)}) %collective-permute-start) | collective-permute-done | bytes 102432 | tf_op jit(solution)/shard_map/ppermute | solution.py:380
  8.1 0.0 copy-start.1
  8.1 0.6 %copy-done.1 = bf16[400,128]{1,0:T(8,128)(2,1)} copy-done((bf16[400,128]{1,0:T(8,128)(2,1)}, bf16[400,128]{1,0:T(8,128)(2,1)S(1)}, u32[]{:S(2)}) %copy-start.1) | copy-done | bytes 102424
  8.7 7.0 %shard_map.93 = (bf16[192,1024]{1,0:T(8,128)(2,1)}, f32[2,192,128]{2,1,0:T(8,128)}, bf16[1,480,128]{2,1,0:T(8,128)(2,1)}, f32[4,256]{1,0:T(4,128)}) custom-call(bf16[192,1024]{1,0:T(8,128)(2,1)} %q_ref.1, bf16[192,128]{1,0:T(8,128)(2,1)} %k_ref.1, bf16[192,128]{1,0:T(8,128)(2,1)} %v_ref.1, bf16[192,1024]{1,0:T(8,128)(2,1)} %g_ref.1, s32[1,192]{1,0:T(1,128)} %bitcast.9, ...), custom_call_target="tpu_custom_call" | custom-call | tf_op jit(solution)/shard_map/pallas_call | solution.py:394
  15.8 1.8 %collective-permute-start.1 = (bf16[480,128]{1,0:T(8,128)(2,1)}, bf16[480,128]{1,0:T(8,128)(2,1)S(1)}, u32[]{:S(2)}, u32[]{:S(2)}) collective-permute-start(bf16[480,128]{1,0:T(8,128)(2,1)} %bitcast.10), channel_id=1, source_target_pairs={{0,4},{4,0},{1,5},{5,1},{2,6},{6,2},{3,7},{7,3},{8,12},{12,8},{9,1... | collective-permute-start | bytes 368648 | tf_op jit(solution)/shard_map/ppermute | solution.py:380
  17.5 3.3 %collective-permute-done.1 = bf16[480,128]{1,0:T(8,128)(2,1)S(1)} collective-permute-done((bf16[480,128]{1,0:T(8,128)(2,1)}, bf16[480,128]{1,0:T(8,128)(2,1)S(1)}, u32[]{:S(2)}, u32[]{:S(2)}) %collective-permute-start.1) | collective-permute-done | bytes 122912 | tf_op jit(solution)/shard_map/ppermute | solution.py:380
  20.9 0.0 copy-start
  20.9 0.6 %copy-done = bf16[480,128]{1,0:T(8,128)(2,1)} copy-done((bf16[480,128]{1,0:T(8,128)(2,1)}, bf16[480,128]{1,0:T(8,128)(2,1)S(1)}, u32[]{:S(2)}) %copy-start) | copy-done | bytes 122904
  21.5 1.6 %shard_map.94 = (bf16[192,128]{1,0:T(8,128)(2,1)}, bf16[192,128]{1,0:T(8,128)(2,1)}, f32[1,16]{1,0:T(1,128)}) custom-call(f32[2,192,128]{2,1,0:T(8,128)} %get-tuple-element.12.own_ref, bf16[1,480,128]{2,1,0:T(8,128)(2,1)} %bitcast.7, f32[4,256]{1,0:T(4,128)} %get-tuple-element.14.sinks_ref), custom_call_target="tpu_custom_call" | custom-call | tf_op jit(solution)/shard_map/pallas_call | solution.py:415
  (1 shorter events, 0.0 us)
Async XLA Ops:
  2.2 5.9 %collective-permute-start = (bf16[400,128]{1,0:T(8,128)(2,1)S(1)}, bf16[400,128]{1,0:T(8,128)(2,1)S(1)}, u32[]{:S(2)}, u32[]{:S(2)}) collective-permute-start(bf16[400,128]{1,0:T(8,128)(2,1)S(1)} %fusion.1), channel_id=1, source_target_pairs={{0,4},{4,0},{1,5},{5,1},{2,6},{6,2},{3,7},{7,3},{8,12},{12,8},{9,1... | collective-permute-start | bytes 307208 | tf_op jit(solution)/shard_map/ppermute | solution.py:380
  8.1 0.6 %copy-start.1 = (bf16[400,128]{1,0:T(8,128)(2,1)}, bf16[400,128]{1,0:T(8,128)(2,1)S(1)}, u32[]{:S(2)}) copy-start(bf16[400,128]{1,0:T(8,128)(2,1)S(1)} %collective-permute-done) | copy-start | bytes 307204
  15.8 5.1 %collective-permute-start.1 = (bf16[480,128]{1,0:T(8,128)(2,1)}, bf16[480,128]{1,0:T(8,128)(2,1)S(1)}, u32[]{:S(2)}, u32[]{:S(2)}) collective-permute-start(bf16[480,128]{1,0:T(8,128)(2,1)} %bitcast.10), channel_id=1, source_target_pairs={{0,4},{4,0},{1,5},{5,1},{2,6},{6,2},{3,7},{7,3},{8,12},{12,8},{9,1... | collective-permute-start | bytes 368648 | tf_op jit(solution)/shard_map/ppermute | solution.py:380
  20.9 0.6 %copy-start = (bf16[480,128]{1,0:T(8,128)(2,1)}, bf16[480,128]{1,0:T(8,128)(2,1)S(1)}, u32[]{:S(2)}) copy-start(bf16[480,128]{1,0:T(8,128)(2,1)S(1)} %collective-permute-done.1) | copy-start | bytes 368644

commit v2 on v0

v2 whole, which is shorter than its diff:
```python
import functools

import jax
import jax.numpy as jnp
from jax import lax
from jax.experimental import pallas as pl
from jax.experimental.pallas import tpu as pltpu
from jax.sharding import PartitionSpec as P

HEAD_SIZE = 64
LANES = 128
BLOCK = 64
NEG = -1e30
F32 = jnp.float32
BF16 = jnp.bfloat16
SCALE = HEAD_SIZE ** (-0.5)


def dot(left, right, left_dim, right_dim):
    return lax.dot_general(
        left, right, (((left_dim,), (right_dim,)), ((), ())), preferred_element_type=F32
    )


def join(parts, axis=0):
    return parts[0] if len(parts) == 1 else jnp.concatenate(parts, axis=axis)


def over_tiles(count, body, carry):
    if count == 1:
        return body(0, carry)
    return lax.fori_loop(0, count, body, carry)


class Keep:
    def __init__(self, ref, count):
        self.ref, self.inline = ref, count == 1

    def put(self, tile, value):
        if self.inline:
            self.value = value
        else:
            self.ref[tile] = value

    def get(self, tile):
        return self.value if self.inline else self.ref[tile]


class Sizes:
    def __init__(self, queries, keys, ctx_size):
        self.length = queries.shape[0]
        self.kv_heads = keys.shape[1] // HEAD_SIZE
        self.pairs = queries.shape[1] // keys.shape[1] // 2
        self.width = self.pairs * BLOCK
        self.blocks = self.length // BLOCK
        self.remote = ctx_size - 1
        self.cols = keys.shape[1]
        self.near = 2 * BLOCK * self.blocks * (self.blocks + 1) // 2
        self.stats = self.kv_heads * self.blocks * 2
        self.seg_rows = -(-self.length // LANES)
        self.slices = self.width // LANES
        self.tall = 2 * self.length + 16 * 3 * self.slices

    def near_at(self, block):
        return slice(BLOCK * block * (block + 1), BLOCK * (block + 1) * (block + 2))

    def stat(self, head, block, half):
        return (head * self.blocks + block) * 2 + half

    def rows(self, block):
        return slice(block * BLOCK, (block + 1) * BLOCK)

    def lanes(self, head, pair):
        at = (head * self.pairs + pair) * LANES
        return slice(at, at + LANES)

    def span(self, head):
        at = head // 2 * LANES
        return slice(at, at + LANES)

    def stack(self, ref, head, block):
        return join([ref[self.rows(block), self.lanes(head, p)] for p in range(self.pairs)])


def columns(row):
    return jnp.broadcast_to(row, (LANES, row.shape[1])).T


def split_halves(block, local):
    lane = lax.broadcasted_iota(jnp.int32, block.shape, 1)
    wide = block.astype(F32)
    turned = pltpu.roll(wide, HEAD_SIZE, 1)
    low = lane < HEAD_SIZE
    zero = jnp.zeros_like(wide)
    if local == 0:
        parts = (jnp.where(low, wide, zero), jnp.where(low, zero, turned))
    else:
        parts = (jnp.where(low, turned, zero), jnp.where(low, zero, wide))
    return [part.astype(BF16) for part in parts]


def seg_features(seg_col, blocked):
    lane = lax.broadcasted_iota(jnp.int32, seg_col.shape, 1)
    other = (lane - BLOCK) != seg_col.astype(jnp.int32)
    if blocked is not None:
        other = other | blocked
    return jnp.where((lane >= BLOCK) & other, NEG, 0.0)


def merge_heads(parts):
    lane = lax.broadcasted_iota(jnp.int32, parts[0][0].shape, 1)
    low = lane < HEAD_SIZE
    (first_low, first_high), (second_low, second_high) = parts
    straight = jnp.where(low, first_low, second_high)
    crossed = jnp.where(low, second_low, first_high)
    return straight + pltpu.roll(crossed, HEAD_SIZE, 1)


def halves(array):
    size = array.shape[0] // 2
    return array[:size], array[size:]


def spread(pair_of_rows, size):
    width = pair_of_rows[0].shape[1]
    return join([jnp.broadcast_to(r, (size, width)) for r in pair_of_rows])


def sink_row(sz, sink_ref, head, half):
    lane = lax.broadcasted_iota(jnp.int32, (1, sz.width), 1)
    line = jnp.zeros((1, sz.width), F32)
    for pair in range(sz.pairs):
        value = sink_ref[head * 2 * sz.pairs + 2 * pair + half]
        line = jnp.where(lane // BLOCK == pair, value, line)
    return line


def pack_kernel(sz, k_ref, v_ref, seg_ref, out_ref, line_ref, k_sem, v_sem, seg_sem):
    seg_copy = pltpu.make_async_copy(seg_ref, line_ref, seg_sem)
    seg_copy.start()
    k_copy = pltpu.make_async_copy(k_ref, out_ref.at[pl.ds(0, sz.length)], k_sem)
    v_copy = pltpu.make_async_copy(v_ref, out_ref.at[pl.ds(sz.length, sz.length)], v_sem)
    k_copy.start()
    v_copy.start()
    seg_copy.wait()
    line = line_ref[...].astype(F32).astype(BF16)
    for i in range(sz.seg_rows):
        count = min(LANES, sz.length - i * LANES)
        at = 2 * sz.length + i
        out_ref[at : at + 1, :count] = line[:, i * LANES : i * LANES + count]
    k_copy.wait()
    v_copy.wait()


def seg_columns(sz, lines):
    lines = lines.astype(F32)
    parts = [columns(lines[i : i + 1, :LANES]) for i in range(sz.seg_rows)]
    return join(parts)[: sz.length]


def near_kernel(
    sz, q_hbm, g_hbm, sink_hbm, own_ref,
    q_ref, g_ref, e_ref, dp_ref, top_ref, mass_ref, feat_ref, sink_rows_ref,
    sink_ref, q_sem, g_sem, sink_sem,
):
    q_copy = pltpu.make_async_copy(q_hbm, q_ref, q_sem)
    g_copy = pltpu.make_async_copy(g_hbm, g_ref, g_sem)
    sink_copy = pltpu.make_async_copy(sink_hbm, sink_ref, sink_sem)
    sink_copy.start()
    q_copy.start()
    g_copy.start()
    shape = (sz.length, LANES)
    length = sz.length
    seg_col = seg_columns(sz, own_ref[2 * length :])
    lane = lax.broadcasted_iota(jnp.int32, shape, 1)
    inner = lax.broadcasted_iota(jnp.int32, shape, 0) % BLOCK
    key_seg = seg_features(seg_col, None)
    key_plain = key_seg.astype(BF16)
    key_diag = jnp.where(lane == inner, 1.0, key_seg).astype(BF16)
    same = (lane - BLOCK) == seg_col.astype(jnp.int32)
    query_feat = jnp.where(
        lane < BLOCK, jnp.where(lane > inner, NEG, 0.0), jnp.where(same, 1.0, 0.0)
    ).astype(BF16)
    feat_ref[...] = query_feat
    sink_copy.wait()
    q_copy.wait()
    g_copy.wait()

    for head in range(sz.kv_heads):
        keys = split_halves(own_ref[:length, sz.span(head)].astype(F32) * SCALE, head % 2)
        values = split_halves(own_ref[length : 2 * length, sz.span(head)], head % 2)
        sinks = [sink_row(sz, sink_ref, head, half) for half in range(2)]
        for half in range(2):
            sink_rows_ref[2 * head + half : 2 * head + half + 1] = sinks[half]
        for block in range(sz.blocks):
            count = (block + 1) * BLOCK
            rows = sz.rows(block)
            q_wide = join(
                [sz.stack(q_ref, head, block), join([query_feat[rows]] * sz.pairs)], 1
            )
            feats = join(([key_plain[: count - BLOCK]] if block else []) + [key_diag[rows]])
            key_wide = join([join([part[:count] for part in keys]), join([feats, feats])], 1)
            scores = dot(key_wide, q_wide, 1, 1)
            tops = [
                jnp.maximum(jnp.max(part, axis=0, keepdims=True), sinks[half])
                for half, part in enumerate(halves(scores))
            ]
            weight = jnp.exp(scores - spread(tops, count))
            at = sz.near_at(block)
            e_ref[head, at] = weight
            for half, part in enumerate(halves(weight)):
                r = sz.stat(head, block, half)
                top_ref[r : r + 1] = tops[half]
                mass_ref[r : r + 1] = jnp.exp(sinks[half] - tops[half]) + jnp.sum(
                    part, axis=0, keepdims=True
                )
            dp_ref[head, at] = dot(
                join([part[:count] for part in values]), sz.stack(g_ref, head, block), 1, 1
            )


def far_kernel(
    sz, ctx_axis, q_ref, g_ref, far_ref, sink_rows_ref, e_ref, dp_ref, top_ref, mass_ref, feat_ref,
    part_ref, ds_ref, ratio_ref, delta_ref, sinks_out_ref,
    s_keep, dp_keep, p_keep, feat_keep,
):
    length, remote = sz.length, sz.remote
    place = lax.axis_index(ctx_axis)
    query_feat = feat_ref[...]
    far_feat = Keep(feat_keep, remote)

    def make_feat(tile, carry):
        far_col = seg_columns(sz, far_ref[tile][2 * length :])
        gone = jnp.full((length, LANES), place - 1 - tile) < 0
        far_feat.put(tile, seg_features(far_col, gone).astype(BF16))
        return carry

    over_tiles(remote, make_feat, 0)
    sums = {}

    for head in range(sz.kv_heads):
        span, local = sz.span(head), head % 2
        q_rows = [sz.stack(q_ref, head, block) for block in range(sz.blocks)]
        g_rows = [sz.stack(g_ref, head, block) for block in range(sz.blocks)]
        sinks = [sink_rows_ref[2 * head + half : 2 * head + half + 1] for half in range(2)]
        sink_sums = [0.0, 0.0]
        far_p = [Keep(p_keep.at[block], remote) for block in range(sz.blocks)]
        far_ds = [Keep(ds_ref.at[head, block], remote) for block in range(sz.blocks)]

        def far_keys(tile):
            return join(split_halves(far_ref[tile, :length, span].astype(F32) * SCALE, local))

        def far_values(tile):
            return join(split_halves(far_ref[tile, length : 2 * length, span], local))

        if remote == 1:
            keys_here, values_here = far_keys(0), far_values(0)
            far_keys, far_values = (lambda tile: keys_here), (lambda tile: values_here)

        for block in range(sz.blocks):
            count = (block + 1) * BLOCK
            q_wide = join([q_rows[block], join([query_feat[sz.rows(block)]] * sz.pairs)], 1)
            g_stack = g_rows[block]
            far_s, far_dp = Keep(s_keep, remote), Keep(dp_keep, remote)
            stat = [sz.stat(head, block, half) for half in range(2)]
            near_tops = [top_ref[r : r + 1] for r in stat]

            def score_far(tile, carry):
                feats = far_feat.get(tile)
                wide = join([far_keys(tile), join([feats, feats])], 1)
                scores = dot(wide, q_wide, 1, 1)
                far_s.put(tile, scores)
                return tuple(
                    jnp.maximum(c, jnp.max(part, axis=0, keepdims=True))
                    for c, part in zip(carry, halves(scores))
                )

            tops = over_tiles(remote, score_far, tuple(near_tops))
            shrink = [jnp.exp(near_tops[half] - tops[half]) for half in range(2)]
            mass = tuple(mass_ref[r : r + 1] * s for r, s in zip(stat, shrink))

            def mass_far(tile, carry):
                weight = jnp.exp(far_s.get(tile) - spread(tops, length))
                far_s.put(tile, weight)
                return tuple(
                    c + jnp.sum(part, axis=0, keepdims=True)
                    for c, part in zip(carry, halves(weight))
                )

            mass = over_tiles(remote, mass_far, mass)
            inverse = [1.0 / m for m in mass]
            ratio = [s * i for s, i in zip(shrink, inverse)]
            at = sz.near_at(block)
            near_half = (e_ref[head, at] * spread(ratio, count)).astype(BF16)
            prod = near_half.astype(F32) * dp_ref[head, at]
            delta = tuple(jnp.sum(part, axis=0, keepdims=True) for part in halves(prod))

            def delta_far(tile, carry):
                prob = far_s.get(tile) * spread(inverse, length)
                far_s.put(tile, prob)
                rounded = prob.astype(BF16)
                far_p[block].put(tile, rounded)
                dprob = dot(far_values(tile), g_stack, 1, 1)
                far_dp.put(tile, dprob)
                return tuple(
                    c + jnp.sum(part, axis=0, keepdims=True)
                    for c, part in zip(carry, halves(rounded.astype(F32) * dprob))
                )

            delta = over_tiles(remote, delta_far, delta)
            for half in range(2):
                sink_prob = jnp.exp(sinks[half] - tops[half]) * inverse[half]
                sink_sums[half] = sink_sums[half] - sink_prob * delta[half]
                ratio_ref[stat[half] : stat[half] + 1] = ratio[half]
                delta_ref[stat[half] : stat[half] + 1] = delta[half]

            def dscore_far(tile, carry):
                dscore = far_s.get(tile) * (far_dp.get(tile) - spread(delta, length))
                dscore = dscore.astype(BF16)
                far_ds[block].put(tile, dscore)
                if remote == 1:
                    ds_ref[head, block, tile] = dscore
                return carry

            over_tiles(remote, dscore_far, 0)

        for half in range(2):
            sinks_out_ref[2 * head + half : 2 * head + half + 1, :] = sink_sums[half]
        q_all, g_all = join(q_rows), join(g_rows)

        def far_sum(tile, carry):
            for which, parts, right in ((0, far_ds, q_all), (1, far_p, g_all)):
                total = dot(join([part.get(tile) for part in parts], 1), right, 1, 0)
                if remote == 1:
                    sums[which, local] = halves(total)
                else:
                    at = slice(which * length, (which + 1) * length)
                    lane = lax.broadcasted_iota(jnp.int32, (length, LANES), 1)
                    low = lane < HEAD_SIZE
                    a, b = halves(total)
                    turned = pltpu.roll(jnp.where(low, a, b), HEAD_SIZE, 1)
                    both = ((a if local == 0 else b) + turned) * (SCALE if which == 0 else 1.0)
                    keep = low if local == 0 else ~low
                    part_ref[tile, at, span] = jnp.where(
                        keep, both.astype(BF16), part_ref[tile, at, span]
                    )
            return carry

        over_tiles(remote, far_sum, 0)
        if remote == 1 and local == 1:
            for which, factor in ((0, SCALE), (1, 1.0)):
                merged = merge_heads([sums[which, 0], sums[which, 1]]) * factor
                part_ref[0, which * length : (which + 1) * length, span] = merged.astype(BF16)

    rest = sinks_out_ref[...]
    for i in range(3):
        piece = rest.astype(BF16)
        rest = rest - piece.astype(F32)
        for tile in range(remote):
            for j in range(sz.slices):
                at = 2 * length + 16 * (i * sz.slices + j)
                part_ref[tile, at : at + 2 * sz.kv_heads, :LANES] = piece[
                    :, j * LANES : (j + 1) * LANES
                ]


def grad_kernel(
    sz, q_ref, own_in_ref, g_ref, far_ref, e_ref, dp_ref, ratio_ref, delta_ref, ds_ref,
    dq_ref, own_ref,
):
    length, remote = sz.length, sz.remote
    sums = {}
    for head in range(sz.kv_heads):
        span, local = sz.span(head), head % 2
        keys = split_halves(own_in_ref[:length, span].astype(F32) * SCALE, local)
        p_near, ds_near, q_rows, g_rows = [], [], [], []

        def far_keys(tile):
            return join(split_halves(far_ref[tile, :length, span].astype(F32) * SCALE, local))

        if remote == 1:
            keys_here = far_keys(0)
            far_keys = lambda tile: keys_here

        for block in range(sz.blocks):
            count = (block + 1) * BLOCK
            at = sz.near_at(block)
            q_rows.append(sz.stack(q_ref, head, block))
            g_rows.append(sz.stack(g_ref, head, block))
            stat = [sz.stat(head, block, half) for half in range(2)]
            ratio = [ratio_ref[r : r + 1] for r in stat]
            delta = [delta_ref[r : r + 1] for r in stat]
            prob = e_ref[head, at] * spread(ratio, count)
            p_near.append(prob.astype(BF16))
            dscore = (prob * (dp_ref[head, at] - spread(delta, count))).astype(BF16)
            ds_near.append(dscore)
            dq = dot(dscore, join([part[:count] for part in keys]), 0, 0)

            def dq_far(tile, carry):
                return carry + dot(ds_ref[head, block, tile], far_keys(tile), 0, 0)

            dq = over_tiles(remote, dq_far, dq)
            for pair in range(sz.pairs):
                dq_ref[sz.rows(block), sz.lanes(head, pair)] = dq[
                    pair * BLOCK : (pair + 1) * BLOCK
                ].astype(BF16)

        for which, parts, right in ((0, ds_near, q_rows), (1, p_near, g_rows)):
            out = [[], []]
            for kb in range(sz.blocks):
                left = []
                for block in range(kb, sz.blocks):
                    left.append(join([half[sz.rows(kb)] for half in halves(parts[block])]))
                for half, total in enumerate(halves(dot(join(left, 1), join(right[kb:]), 1, 0))):
                    out[half].append(total)
            sums[which, local] = [join(o) for o in out]
        if local == 1:
            own_ref[0, :, span] = merge_heads([sums[0, 0], sums[0, 1]]) * SCALE
            own_ref[1, :, span] = merge_heads([sums[1, 0], sums[1, 1]])


def last_kernel(sz, own_ref, back_ref, sinks_ref, dk_ref, dv_ref, out_ref):
    length = sz.length
    totals = [own_ref[0], own_ref[1]]
    sink = sinks_ref[...]
    count = sink.shape[0]
    for tile in range(sz.remote):
        for which in range(2):
            at = slice(which * length, (which + 1) * length)
            totals[which] = totals[which] + back_ref[tile, at].astype(F32)
        rest = jnp.zeros_like(sink)
        for i in range(3):
            pieces = []
            for j in range(sz.slices):
                at = 2 * length + 16 * (i * sz.slices + j)
                pieces.append(back_ref[tile, at : at + count, :LANES].astype(F32))
            rest = rest + join(pieces, 1)
        sink = sink + rest
    dk_ref[...] = totals[0].astype(BF16)
    dv_ref[...] = totals[1].astype(BF16)
    lane = lax.broadcasted_iota(jnp.int32, sink.shape, 1)
    out_lane = lax.broadcasted_iota(jnp.int32, out_ref.shape, 1)
    line = jnp.zeros(out_ref.shape, F32)
    for pair in range(sz.pairs):
        sums = jnp.sum(jnp.where(lane // BLOCK == pair, sink, 0.0), axis=1, keepdims=True)
        for r in range(count):
            at = (r // 2) * 2 * sz.pairs + 2 * pair + r % 2
            line = jnp.where(out_lane == at, sums[r : r + 1], line)
    out_ref[...] = line


def on_device(ctx_size, queries, keys, values, grad_out, segments, sinks):
    sz = Sizes(queries, keys, ctx_size)
    length, width, remote = sz.length, sz.width, sz.remote
    vmem = pl.BlockSpec(memory_space=pltpu.VMEM)
    hbm = pl.BlockSpec(memory_space=pltpu.HBM)
    shape = jax.ShapeDtypeStruct
    seg_line = segments.reshape(1, length)
    small = remote == 1

    def stay(array):
        return pltpu.with_memory_space_constraint(array, pltpu.HBM)

    def params(mib):
        return pltpu.CompilerParams(vmem_limit_bytes=mib << 20)

    def cost(flops):
        return pl.CostEstimate(flops=flops, bytes_accessed=1 << 20, transcendentals=0)

    tile_flops = 4 * queries.shape[0] * queries.shape[1] * length

    packed = pl.pallas_call(
        functools.partial(pack_kernel, sz),
        out_shape=shape((2 * length + 16, sz.cols), BF16),
        in_specs=[hbm, hbm, hbm],
        out_specs=vmem,
        scratch_shapes=[pltpu.VMEM((1, length), jnp.int32)] + [pltpu.SemaphoreType.DMA] * 3,
        compiler_params=params(4),
    )(stay(keys), stay(values), stay(seg_line))

    def turn(array, shift):
        order = [(i, (i + shift) % ctx_size) for i in range(ctx_size)]
        return lax.ppermute(array, "ctx", order)

    far = jnp.stack([turn(packed, s) for s in range(1, ctx_size)])

    q_here, g_here, weights, dprob, tops, mass, feats, sink_in = pl.pallas_call(
        functools.partial(near_kernel, sz),
        out_shape=(
            shape(queries.shape, BF16),
            shape(grad_out.shape, BF16),
            shape((sz.kv_heads, sz.near, width), F32),
            shape((sz.kv_heads, sz.near, width), F32),
            shape((sz.stats, width), F32),
            shape((sz.stats, width), F32),
            shape((length, LANES), BF16),
            shape((2 * sz.kv_heads, width), F32),
        ),
        in_specs=[hbm, hbm, hbm, vmem],
        out_specs=(vmem,) * 8,
        scratch_shapes=[pltpu.SMEM(sinks.shape, F32)] + [pltpu.SemaphoreType.DMA] * 3,
        compiler_params=params(16),
        cost_estimate=cost(2 * tile_flops),
    )(stay(queries), stay(grad_out), stay(sinks), packed)

    part, ds_far, ratio, delta, sink_rows = pl.pallas_call(
        functools.partial(far_kernel, sz, "ctx"),
        out_shape=(
            shape((remote, sz.tall, sz.cols), BF16),
            shape((sz.kv_heads, sz.blocks, remote, 2 * length, width), BF16),
            shape((sz.stats, width), F32),
            shape((sz.stats, width), F32),
            shape((2 * sz.kv_heads, width), F32),
        ),
        in_specs=[vmem] * 9,
        out_specs=(vmem,) * 5,
        scratch_shapes=[
            pltpu.VMEM((1, 8, LANES) if small else (remote, 2 * length, width), F32),
            pltpu.VMEM((1, 8, LANES) if small else (remote, 2 * length, width), F32),
            pltpu.VMEM(
                (sz.blocks, 1, 16, LANES) if small else (sz.blocks, remote, 2 * length, width),
                BF16,
            ),
            pltpu.VMEM((1, 16, LANES) if small else (remote, length, LANES), BF16),
        ],
        compiler_params=params(16 if small else 60),
        cost_estimate=cost(4 * tile_flops),
    )(q_here, g_here, far, sink_in, weights, dprob, tops, mass, feats)

    back = jnp.stack([turn(part[s - 1], -s) for s in range(1, ctx_size)])

    dq, own = pl.pallas_call(
        functools.partial(grad_kernel, sz),
        out_shape=(shape(queries.shape, BF16), shape((2,) + keys.shape, F32)),
        in_specs=[vmem] * 9,
        out_specs=(vmem, vmem),
        compiler_params=params(16 if small else 60),
        cost_estimate=cost(4 * tile_flops),
    )(q_here, packed, g_here, far, weights, dprob, ratio, delta, ds_far)

    heads = sinks.shape[0]
    dk, dv, line = pl.pallas_call(
        functools.partial(last_kernel, sz),
        out_shape=(shape(keys.shape, BF16), shape(values.shape, BF16), shape((1, heads), F32)),
        in_specs=[vmem, vmem, vmem],
        out_specs=(vmem, vmem, vmem),
        compiler_params=params(8),
    )(own, back, sink_rows)
    return dq, dk, dv, line.reshape(heads)


def solution(mesh):
    rows = P(("dp", "ctx"), "tp")
    return jax.shard_map(
        functools.partial(on_device, mesh.shape["ctx"]),
        mesh=mesh,
        in_specs=(rows, rows, rows, rows, P(("dp", "ctx")), P("tp")),
        out_specs=(rows, rows, rows, P(("dp", "tp"))),
        check_vma=False,
    )
```

time: 125 us -> 15.6 us (0.12)
  blocking collectives: 46.8 us -> 0 us
  local copies, waits for them, and re-layouts: 21.6 us -> 0 us
  matrix products: 14.3 us -> 0 us
  between operations: 14.9 us -> 0.66 us
  waiting for transfers between devices: 15.7 us -> 2.09 us
  other arithmetic: 10.2 us -> 0 us
  Pallas kernels: 0 us -> 7.72 us
  starting transfers between devices: 0.08 us -> 4.9 us
    psum x1 -> x0, blocking collectives: 28.5 us -> none  [on_device(): grad_sinks = lax.psum(sink_term, 'ctx')]
    reduce_scatter x2 -> x0, waiting for transfers between devices: 15 us -> none  [the longest x1 11.8 us: on_device(): lax.psum_scatter(value_buf, 'ctx', scatter_dimension=0, tiled=True)]
    dot_general x7 -> x0, matrix products: 14.3 us -> none  [the longest x2 3.68 us: tile_scores(): lax.dot_general(query_heads, key_block, (((2,), (2,)), ((0,), (0,))), pre...]
    all_gather x2 -> x0, blocking collectives: 13 us -> none  [the longest x1 8.27 us: on_device(): lax.all_gather(values, 'ctx', axis=0, tiled=True)]
    pallas_call x0 -> x5, Pallas kernels: none -> 7.72 us  [the longest x1 2.31 us: on_device(): pl.pallas_call(functools.partial(far_kernel, sz, 'ctx'), out_shape=(shape...]
    unnamed x1 -> x0, blocking collectives: 5.25 us -> none
    another operation x10 -> x0, local copies, waits for them, and re-layouts: 5.22 us -> none  [the longest x6 2.78 us: tile_scores(): allowed = jnp.tile(allowed, (query_group, 1))[None]]
    unnamed x21 -> x0, local copies, waits for them, and re-layouts: 5.05 us -> none
  transfers between devices with their start and end apart: 2 -> 2, of which waited for: 2 -> 2; matrix products, arithmetic and copies ran while one was open for 4% -> 0% of each run, Pallas kernels for 0% -> 25%
where the time goes in v2:
time: 15.6 us; the launch traced here: 15.4 us
  Pallas kernels  7.72 us (49%)
  starting transfers between devices  4.9 us (31%)
  waiting for transfers between devices  2.09 us (13%)
  between operations  0.66 us (4%)
    ppermute x2, starting transfers between devices, turn(): return lax.ppermute(array, 'ctx', order)  4.9 us
    pallas_call x1, Pallas kernels, on_device(): pl.pallas_call(functools.partial(far_kernel, sz, 'ctx'), out_shape=(shape...  2.31 us
    ppermute x2, waiting for transfers between devices, turn(): return lax.ppermute(array, 'ctx', order)  2.09 us
    pallas_call x1, Pallas kernels, on_device(): pl.pallas_call(functools.partial(grad_kernel, sz), out_shape=(shape(queri...  2.03 us
    pallas_call x1, Pallas kernels, on_device(): pl.pallas_call(functools.partial(near_kernel, sz), out_shape=(shape(queri...  1.86 us
    pallas_call x1, Pallas kernels, on_device(): pl.pallas_call(functools.partial(pack_kernel, sz), out_shape=shape((2 * l...  0.87 us
    pallas_call x1, Pallas kernels, on_device(): pl.pallas_call(functools.partial(last_kernel, sz), out_shape=(shape(keys....  0.65 us
  transfers between devices with their start and end apart: 2, of which 2 were waited for; matrix products, arithmetic and copies ran while one was open for 0% of the time, Pallas kernels for 25%

profile of v2, /device:TPU:0, one launch (start us, length us, event | category | flops | bytes accessed | tf_op | source)
XLA Modules:
  0.0 15.4 jit_solution(13054759364607856050)
XLA Ops:
  0.6 0.9 %shard_map.93.own_ref.own_in_ref = bf16[400,128]{1,0:T(8,128)(2,1)S(1)} custom-call(bf16[192,128]{1,0:T(8,128)(2,1)} %k_ref.1, bf16[192,128]{1,0:T(8,128)(2,1)} %v_ref.1, s32[1,192]{1,0:T(1,128)} %bitcast.9), custom_call_target="tpu_custom_call" | custom-call | tf_op jit(solution)/shard_map/pallas_call | solution.py:472
  1.5 3.1 %collective-permute-start = (bf16[400,128]{1,0:T(8,128)(2,1)S(1)}, bf16[400,128]{1,0:T(8,128)(2,1)S(1)}, u32[]{:S(2)}, u32[]{:S(2)}) collective-permute-start(bf16[400,128]{1,0:T(8,128)(2,1)S(1)} %shard_map.93.own_ref.own_in_ref), channel_id=1, source_target_pairs={{0,4},{4,0},{1,5},{5,1},{2,6},{6,2},{3,7},{7,3},{8,12},{12,8},{9,1... | collective-permute-start | bytes 307208 | tf_op jit(solution)/shard_map/ppermute | solution.py:483
  4.6 1.9 %shard_map.94 = (bf16[192,1024]{1,0:T(8,128)(2,1)S(1)}, bf16[192,1024]{1,0:T(8,128)(2,1)S(1)}, f32[2,768,256]{2,1,0:T(8,128)S(1)}, f32[2,768,256]{2,1,0:T(8,128)...) custom-call(bf16[192,1024]{1,0:T(8,128)(2,1)} %q_hbm.1, ...), custom_call_target="tpu_custom_call" | custom-call | flops 301989888 | bytes 1048576 | tf_op jit(solution)/shard_map/pallas_call | solution.py:487
  6.4 1.0 %collective-permute-done = bf16[400,128]{1,0:T(8,128)(2,1)S(1)} collective-permute-done((bf16[400,128]{1,0:T(8,128)(2,1)S(1)}, bf16[400,128]{1,0:T(8,128)(2,1)S(1)}, u32[]{:S(2)}, u32[]{:S(2)}) %collective-permute-start) | collective-permute-done | bytes 102432 | tf_op jit(solution)/shard_map/ppermute | solution.py:483
  7.4 2.3 %shard_map.95 = (bf16[1,480,128]{2,1,0:T(8,128)(2,1)S(1)}, bf16[2,3,1,384,256]{4,3,2,1,0:T(8,128)(2,1)S(1)}, f32[12,256]{1,0:T(8,128)S(1)}, f32[12,256]{1,0:T(8,128)S(1)}, f32[4,256]{1,0:T(4,128)S(1)}) custom-call(bf16[192,1024]{1,0:T(8,128)(2,1)S(1)} %get-tuple-element.22.q_ref, bf16[192,1024]{1,0:T(8,128)(2,1)S(1)} %get-tuple-element.23.g_ref, ...), custom_call_target="tpu_custom_call" | custom-call | flops 603979776 | bytes 1048576 | tf_op jit(solution)/shard_map/pallas_call | solution.py:506
  9.8 1.8 %collective-permute-start.1 = (bf16[480,128]{1,0:T(8,128)(2,1)S(1)}, bf16[480,128]{1,0:T(8,128)(2,1)S(1)}, u32[]{:S(2)}, u32[]{:S(2)}) collective-permute-start(bf16[480,128]{1,0:T(8,128)(2,1)S(1)} %bitcast.8), channel_id=1, source_target_pairs={{0,4},{4,0},{1,5},{5,1},{2,6},{6,2},{3,7},{7,3},{8,12},{12,8},{9,1... | collective-permute-start | bytes 368648 | tf_op jit(solution)/shard_map/ppermute | solution.py:483
  11.6 2.0 %shard_map.96 = (bf16[192,1024]{1,0:T(8,128)(2,1)}, f32[2,192,128]{2,1,0:T(8,128)S(1)}) custom-call(bf16[192,1024]{1,0:T(8,128)(2,1)S(1)} %get-tuple-element.22.q_ref, bf16[400,128]{1,0:T(8,128)(2,1)S(1)} %shard_map.93.own_ref.own_in_ref, bf16[192,1024]{1,0:T(8,128)(2,1)S(1)} %get-tuple-element.23.g_ref, bf16[1,400,128]{2,1,0:T(8,128)(2,1)S(1)} %bitcast.6, ...), custom_call_target="tpu_custom_call" | custom-call | flops 603979776 | bytes 1048576 | tf_op jit(solution)/shard_map/pallas_call | solution.py:532
  13.6 1.1 %collective-permute-done.1 = bf16[480,128]{1,0:T(8,128)(2,1)S(1)} collective-permute-done((bf16[480,128]{1,0:T(8,128)(2,1)S(1)}, bf16[480,128]{1,0:T(8,128)(2,1)S(1)}, u32[]{:S(2)}, u32[]{:S(2)}) %collective-permute-start.1) | collective-permute-done | bytes 122912 | tf_op jit(solution)/shard_map/ppermute | solution.py:483
  14.7 0.7 %shard_map.97 = (bf16[192,128]{1,0:T(8,128)(2,1)}, bf16[192,128]{1,0:T(8,128)(2,1)}, f32[1,16]{1,0:T(1,128)}) custom-call(f32[2,192,128]{2,1,0:T(8,128)S(1)} %get-tuple-element.34.own_ref, bf16[1,480,128]{2,1,0:T(8,128)(2,1)S(1)} %bitcast.7, f32[4,256]{1,0:T(4,128)S(1)} %get-tuple-element.36.sinks_ref), custom_call_target="tpu_custom_call" | custom-call | tf_op jit(solution)/shard_map/pallas_call | solution.py:542
Async XLA Ops:
  1.5 5.9 %collective-permute-start = (bf16[400,128]{1,0:T(8,128)(2,1)S(1)}, bf16[400,128]{1,0:T(8,128)(2,1)S(1)}, u32[]{:S(2)}, u32[]{:S(2)}) collective-permute-start(bf16[400,128]{1,0:T(8,128)(2,1)S(1)} %shard_map.93.own_ref.own_in_ref), channel_id=1, source_target_pairs={{0,4},{4,0},{1,5},{5,1},{2,6},{6,2},{3,7},{7,3},{8,12},{12,8},{9,1... | collective-permute-start | bytes 307208 | tf_op jit(solution)/shard_map/ppermute | solution.py:483
  9.8 4.9 %collective-permute-start.1 = (bf16[480,128]{1,0:T(8,128)(2,1)S(1)}, bf16[480,128]{1,0:T(8,128)(2,1)S(1)}, u32[]{:S(2)}, u32[]{:S(2)}) collective-permute-start(bf16[480,128]{1,0:T(8,128)(2,1)S(1)} %bitcast.8), channel_id=1, source_target_pairs={{0,4},{4,0},{1,5},{5,1},{2,6},{6,2},{3,7},{7,3},{8,12},{12,8},{9,1... | collective-permute-start | bytes 368648 | tf_op jit(solution)/shard_map/ppermute | solution.py:483

commit v3 on v2

--- a/solution.py
+++ b/solution.py
@@ -59,7 +59,8 @@
         self.stats = self.kv_heads * self.blocks * 2
         self.seg_rows = -(-self.length // LANES)
         self.slices = self.width // LANES
-        self.tall = 2 * self.length + 16 * 3 * self.slices
+        self.extra = 3 * self.slices * 2 * self.kv_heads
+        self.tall = 2 * self.length + -(-self.extra // 16) * 16
 
     def near_at(self, block):
         return slice(BLOCK * block * (block + 1), BLOCK * (block + 1) * (block + 2))
@@ -135,21 +136,29 @@
     return line
 
 
-def pack_kernel(sz, k_ref, v_ref, seg_ref, out_ref, line_ref, k_sem, v_sem, seg_sem):
-    seg_copy = pltpu.make_async_copy(seg_ref, line_ref, seg_sem)
-    seg_copy.start()
-    k_copy = pltpu.make_async_copy(k_ref, out_ref.at[pl.ds(0, sz.length)], k_sem)
-    v_copy = pltpu.make_async_copy(v_ref, out_ref.at[pl.ds(sz.length, sz.length)], v_sem)
-    k_copy.start()
-    v_copy.start()
-    seg_copy.wait()
-    line = line_ref[...].astype(F32).astype(BF16)
-    for i in range(sz.seg_rows):
-        count = min(LANES, sz.length - i * LANES)
-        at = 2 * sz.length + i
-        out_ref[at : at + 1, :count] = line[:, i * LANES : i * LANES + count]
-    k_copy.wait()
-    v_copy.wait()
+def pack_kernel(sz, ctx_axis, k_ref, v_ref, seg_ref, out_ref, line_ref, k_sem, v_sem, seg_sem):
+    last = lax.axis_index(ctx_axis) == sz.remote
+
+    @pl.when(last)
+    def _():
+        out_ref[...] = jnp.zeros_like(out_ref)
+
+    @pl.when(jnp.logical_not(last))
+    def _():
+        seg_copy = pltpu.make_async_copy(seg_ref, line_ref, seg_sem)
+        k_copy = pltpu.make_async_copy(k_ref, out_ref.at[pl.ds(0, sz.length)], k_sem)
+        v_copy = pltpu.make_async_copy(v_ref, out_ref.at[pl.ds(sz.length, sz.length)], v_sem)
+        seg_copy.start()
+        k_copy.start()
+        v_copy.start()
+        seg_copy.wait()
+        line = line_ref[...].astype(F32).astype(BF16)
+        for i in range(sz.seg_rows):
+            count = min(LANES, sz.length - i * LANES)
+            at = 2 * sz.length + i
+            out_ref[at : at + 1, :count] = line[:, i * LANES : i * LANES + count]
+        k_copy.wait()
+        v_copy.wait()
 
 
 def seg_columns(sz, lines):
@@ -159,19 +168,24 @@
 
 
 def near_kernel(
-    sz, q_hbm, g_hbm, sink_hbm, own_ref,
-    q_ref, g_ref, e_ref, dp_ref, top_ref, mass_ref, feat_ref, sink_rows_ref,
-    sink_ref, q_sem, g_sem, sink_sem,
+    sz, q_hbm, k_hbm, v_hbm, g_hbm, seg_hbm, sink_hbm, after_ref,
+    q_ref, k_ref, g_ref, e_ref, dp_ref, top_ref, mass_ref, feat_ref, sink_rows_ref,
+    v_ref, seg_ref, sink_ref, sems,
 ):
-    q_copy = pltpu.make_async_copy(q_hbm, q_ref, q_sem)
-    g_copy = pltpu.make_async_copy(g_hbm, g_ref, g_sem)
-    sink_copy = pltpu.make_async_copy(sink_hbm, sink_ref, sink_sem)
-    sink_copy.start()
-    q_copy.start()
-    g_copy.start()
+    del after_ref
+    pairs_of_refs = (
+        (seg_hbm, seg_ref), (sink_hbm, sink_ref), (k_hbm, k_ref),
+        (q_hbm, q_ref), (v_hbm, v_ref), (g_hbm, g_ref),
+    )
+    copies = [
+        pltpu.make_async_copy(a, b, sems.at[i]) for i, (a, b) in enumerate(pairs_of_refs)
+    ]
+    for copy in copies:
+        copy.start()
     shape = (sz.length, LANES)
     length = sz.length
-    seg_col = seg_columns(sz, own_ref[2 * length :])
+    copies[0].wait()
+    seg_col = columns(seg_ref[...].astype(F32))
     lane = lax.broadcasted_iota(jnp.int32, shape, 1)
     inner = lax.broadcasted_iota(jnp.int32, shape, 0) % BLOCK
     key_seg = seg_features(seg_col, None)
@@ -182,13 +196,12 @@
         lane < BLOCK, jnp.where(lane > inner, NEG, 0.0), jnp.where(same, 1.0, 0.0)
     ).astype(BF16)
     feat_ref[...] = query_feat
-    sink_copy.wait()
-    q_copy.wait()
-    g_copy.wait()
+    for copy in copies[1:]:
+        copy.wait()
 
     for head in range(sz.kv_heads):
-        keys = split_halves(own_ref[:length, sz.span(head)].astype(F32) * SCALE, head % 2)
-        values = split_halves(own_ref[length : 2 * length, sz.span(head)], head % 2)
+        keys = split_halves(k_ref[:, sz.span(head)].astype(F32) * SCALE, head % 2)
+        values = split_halves(v_ref[:, sz.span(head)], head % 2)
         sinks = [sink_row(sz, sink_ref, head, half) for half in range(2)]
         for half in range(2):
             sink_rows_ref[2 * head + half : 2 * head + half + 1] = sinks[half]
@@ -358,21 +371,21 @@
         rest = rest - piece.astype(F32)
         for tile in range(remote):
             for j in range(sz.slices):
-                at = 2 * length + 16 * (i * sz.slices + j)
+                at = 2 * length + 2 * sz.kv_heads * (i * sz.slices + j)
                 part_ref[tile, at : at + 2 * sz.kv_heads, :LANES] = piece[
                     :, j * LANES : (j + 1) * LANES
                 ]
 
 
 def grad_kernel(
-    sz, q_ref, own_in_ref, g_ref, far_ref, e_ref, dp_ref, ratio_ref, delta_ref, ds_ref,
+    sz, q_ref, k_ref, g_ref, far_ref, e_ref, dp_ref, ratio_ref, delta_ref, ds_ref,
     dq_ref, own_ref,
 ):
     length, remote = sz.length, sz.remote
     sums = {}
     for head in range(sz.kv_heads):
         span, local = sz.span(head), head % 2
-        keys = split_halves(own_in_ref[:length, span].astype(F32) * SCALE, local)
+        keys = split_halves(k_ref[:, span].astype(F32) * SCALE, local)
         p_near, ds_near, q_rows, g_rows = [], [], [], []
 
         def far_keys(tile):
@@ -432,7 +445,7 @@
         for i in range(3):
             pieces = []
             for j in range(sz.slices):
-                at = 2 * length + 16 * (i * sz.slices + j)
+                at = 2 * length + count * (i * sz.slices + j)
                 pieces.append(back_ref[tile, at : at + count, :LANES].astype(F32))
             rest = rest + join(pieces, 1)
         sink = sink + rest
@@ -470,7 +483,8 @@
     tile_flops = 4 * queries.shape[0] * queries.shape[1] * length
 
     packed = pl.pallas_call(
-        functools.partial(pack_kernel, sz),
+        functools.partial(pack_kernel, sz, "ctx"),
+        name="pack",
         out_shape=shape((2 * length + 16, sz.cols), BF16),
         in_specs=[hbm, hbm, hbm],
         out_specs=vmem,
@@ -484,10 +498,12 @@
 
     far = jnp.stack([turn(packed, s) for s in range(1, ctx_size)])
 
-    q_here, g_here, weights, dprob, tops, mass, feats, sink_in = pl.pallas_call(
+    q_here, k_here, g_here, weights, dprob, tops, mass, feats, sink_in = pl.pallas_call(
         functools.partial(near_kernel, sz),
+        name="near",
         out_shape=(
             shape(queries.shape, BF16),
+            shape(keys.shape, BF16),
             shape(grad_out.shape, BF16),
             shape((sz.kv_heads, sz.near, width), F32),
             shape((sz.kv_heads, sz.near, width), F32),
@@ -496,15 +512,21 @@
             shape((length, LANES), BF16),
             shape((2 * sz.kv_heads, width), F32),
         ),
-        in_specs=[hbm, hbm, hbm, vmem],
-        out_specs=(vmem,) * 8,
-        scratch_shapes=[pltpu.SMEM(sinks.shape, F32)] + [pltpu.SemaphoreType.DMA] * 3,
+        in_specs=[hbm] * 6 + [vmem],
+        out_specs=(vmem,) * 9,
+        scratch_shapes=[
+            pltpu.VMEM(values.shape, BF16),
+            pltpu.VMEM((1, length), jnp.int32),
+            pltpu.SMEM(sinks.shape, F32),
+            pltpu.SemaphoreType.DMA((6,)),
+        ],
         compiler_params=params(16),
         cost_estimate=cost(2 * tile_flops),
-    )(stay(queries), stay(grad_out), stay(sinks), packed)
+    )(*[stay(a) for a in (queries, keys, values, grad_out, seg_line, sinks)], packed)
 
     part, ds_far, ratio, delta, sink_rows = pl.pallas_call(
         functools.partial(far_kernel, sz, "ctx"),
+        name="far",
         out_shape=(
             shape((remote, sz.tall, sz.cols), BF16),
             shape((sz.kv_heads, sz.blocks, remote, 2 * length, width), BF16),
@@ -531,16 +553,18 @@
 
     dq, own = pl.pallas_call(
         functools.partial(grad_kernel, sz),
+        name="grad",
         out_shape=(shape(queries.shape, BF16), shape((2,) + keys.shape, F32)),
         in_specs=[vmem] * 9,
         out_specs=(vmem, vmem),
         compiler_params=params(16 if small else 60),
         cost_estimate=cost(4 * tile_flops),
-    )(q_here, packed, g_here, far, weights, dprob, ratio, delta, ds_far)
+    )(q_here, k_here, g_here, far, weights, dprob, ratio, delta, ds_far)
 
     heads = sinks.shape[0]
     dk, dv, line = pl.pallas_call(
         functools.partial(last_kernel, sz),
+        name="last",
         out_shape=(shape(keys.shape, BF16), shape(values.shape, BF16), shape((1, heads), F32)),
         in_specs=[vmem, vmem, vmem],
         out_specs=(vmem, vmem, vmem),

time: 15.6 us -> 14.8 us (0.949)
  starting transfers between devices: 4.9 us -> 3.85 us
  waiting for transfers between devices: 2.09 us -> 2.3 us
    ppermute x2, starting transfers between devices: 4.9 us -> 3.85 us  [turn(): return lax.ppermute(array, 'ctx', order)]
    ppermute x2, waiting for transfers between devices: 2.09 us -> 2.3 us  [turn(): return lax.ppermute(array, 'ctx', order)]
  transfers between devices with their start and end apart: 2 -> 2, of which waited for: 2 -> 2; matrix products, arithmetic and copies ran while one was open for 0% -> 0% of each run, Pallas kernels for 25% -> 27%
where the time goes in v3:
time: 14.8 us; the launch traced here: 14.6 us
  Pallas kernels  7.79 us (53%)
  starting transfers between devices  3.85 us (26%)
  waiting for transfers between devices  2.3 us (16%)
  between operations  0.65 us (4%)
    ppermute x2, starting transfers between devices, turn(): return lax.ppermute(array, 'ctx', order)  3.85 us
    pallas_call x1, Pallas kernels, on_device(): pl.pallas_call(functools.partial(far_kernel, sz, 'ctx'), name='far', out_...  2.3 us
    ppermute x2, waiting for transfers between devices, turn(): return lax.ppermute(array, 'ctx', order)  2.3 us
    pallas_call x1, Pallas kernels, on_device(): pl.pallas_call(functools.partial(grad_kernel, sz), name='grad', out_shape...  2 us
    pallas_call x1, Pallas kernels, on_device(): pl.pallas_call(functools.partial(near_kernel, sz), name='near', out_shape...  1.95 us
    pallas_call x1, Pallas kernels, on_device(): pl.pallas_call(functools.partial(pack_kernel, sz, 'ctx'), name='pack', ou...  0.88 us
    pallas_call x1, Pallas kernels, on_device(): pl.pallas_call(functools.partial(last_kernel, sz), name='last', out_shape...  0.66 us
  transfers between devices with their start and end apart: 2, of which 2 were waited for; matrix products, arithmetic and copies ran while one was open for 0% of the time, Pallas kernels for 27%

profile of v3, /device:TPU:0, one launch (start us, length us, event | category | flops | bytes accessed | tf_op | source)
XLA Modules:
  0.0 14.6 jit_solution(10609287103076292421)
XLA Ops:
  0.6 0.9 %pack.1.after_ref = bf16[400,128]{1,0:T(8,128)(2,1)S(1)} custom-call(bf16[192,128]{1,0:T(8,128)(2,1)} %k_hbm.1, bf16[192,128]{1,0:T(8,128)(2,1)} %v_hbm.1, s32[1,192]{1,0:T(1,128)} %bitcast.9), custom_call_target="tpu_custom_call" | custom-call | tf_op jit(solution)/shard_map/pack/pallas_call | solution.py:485
  1.5 2.2 %collective-permute-start = (bf16[400,128]{1,0:T(8,128)(2,1)S(1)}, bf16[400,128]{1,0:T(8,128)(2,1)S(1)}, u32[]{:S(2)}, u32[]{:S(2)}) collective-permute-start(bf16[400,128]{1,0:T(8,128)(2,1)S(1)} %pack.1.after_ref), channel_id=1, source_target_pairs={{0,4},{4,0},{1,5},{5,1},{2,6},{6,2},{3,7},{7,3},{8,12},{12,8},{9,1... | collective-permute-start | bytes 307208 | tf_op jit(solution)/shard_map/ppermute | solution.py:497
  3.8 2.0 %near.1 = (bf16[192,1024]{1,0:T(8,128)(2,1)S(1)}, bf16[192,128]{1,0:T(8,128)(2,1)S(1)}, bf16[192,1024]{1,0:T(8,128)(2,1)S(1)}, f32[2,768,256]{2,1,0:T(8,128)S(1)...) custom-call(bf16[192,1024]{1,0:T(8,128)(2,1)} %q_hbm.1, ...), custom_call_target="tpu_custom_call" | custom-call | flops 301989888 | bytes 1048576 | tf_op jit(solution)/shard_map/near/pallas_call | solution.py:501
  5.7 1.1 %collective-permute-done = bf16[400,128]{1,0:T(8,128)(2,1)S(1)} collective-permute-done((bf16[400,128]{1,0:T(8,128)(2,1)S(1)}, bf16[400,128]{1,0:T(8,128)(2,1)S(1)}, u32[]{:S(2)}, u32[]{:S(2)}) %collective-permute-start) | collective-permute-done | bytes 102432 | tf_op jit(solution)/shard_map/ppermute | solution.py:497
  6.9 2.3 %far.1 = (bf16[1,416,128]{2,1,0:T(8,128)(2,1)S(1)}, bf16[2,3,1,384,256]{4,3,2,1,0:T(8,128)(2,1)S(1)}, f32[12,256]{1,0:T(8,128)S(1)}, f32[12,256]{1,0:T(8,128)S(1)}, f32[4,256]{1,0:T(4,128)S(1)}) custom-call(bf16[192,1024]{1,0:T(8,128)(2,1)S(1)} %get-tuple-element.23.q_ref, bf16[192,1024]{1,0:T(8,128)(2,1)S(1)} %get-tuple-element.25.g_ref, ...), custom_call_target="tpu_custom_call" | custom-call | flops 603979776 | bytes 1048576 | tf_op jit(solution)/shard_map/far/pallas_call | solution.py:527
  9.2 1.6 %collective-permute-start.1 = (bf16[416,128]{1,0:T(8,128)(2,1)S(1)}, bf16[416,128]{1,0:T(8,128)(2,1)S(1)}, u32[]{:S(2)}, u32[]{:S(2)}) collective-permute-start(bf16[416,128]{1,0:T(8,128)(2,1)S(1)} %bitcast.8), channel_id=1, source_target_pairs={{0,4},{4,0},{1,5},{5,1},{2,6},{6,2},{3,7},{7,3},{8,12},{12,8},{9,1... | collective-permute-start | bytes 319496 | tf_op jit(solution)/shard_map/ppermute | solution.py:497
  10.8 2.0 %grad.1 = (bf16[192,1024]{1,0:T(8,128)(2,1)}, f32[2,192,128]{2,1,0:T(8,128)S(1)}) custom-call(bf16[192,1024]{1,0:T(8,128)(2,1)S(1)} %get-tuple-element.23.q_ref, bf16[192,128]{1,0:T(8,128)(2,1)S(1)} %get-tuple-element.24.k_ref, bf16[192,1024]{1,0:T(8,128)(2,1)S(1)} %get-tuple-element.25.g_ref, bf16[1,400,128]{2,1,0:T(8,128)(2,1)S(1)} %bitcast.6, ...), custom_call_target="tpu_custom_call" | custom-call | flops 603979776 | bytes 1048576 | tf_op jit(solution)/shard_map/grad/pallas_call | solution.py:554
  12.8 1.2 %collective-permute-done.1 = bf16[416,128]{1,0:T(8,128)(2,1)S(1)} collective-permute-done((bf16[416,128]{1,0:T(8,128)(2,1)S(1)}, bf16[416,128]{1,0:T(8,128)(2,1)S(1)}, u32[]{:S(2)}, u32[]{:S(2)}) %collective-permute-start.1) | collective-permute-done | bytes 106528 | tf_op jit(solution)/shard_map/ppermute | solution.py:497
  13.9 0.7 %last.1 = (bf16[192,128]{1,0:T(8,128)(2,1)}, bf16[192,128]{1,0:T(8,128)(2,1)}, f32[1,16]{1,0:T(1,128)}) custom-call(f32[2,192,128]{2,1,0:T(8,128)S(1)} %get-tuple-element.36.own_ref, bf16[1,416,128]{2,1,0:T(8,128)(2,1)S(1)} %bitcast.7, f32[4,256]{1,0:T(4,128)S(1)} %get-tuple-element.38.sinks_ref), custom_call_target="tpu_custom_call" | custom-call | tf_op jit(solution)/shard_map/last/pallas_call | solution.py:565
Async XLA Ops:
  1.5 5.3 %collective-permute-start = (bf16[400,128]{1,0:T(8,128)(2,1)S(1)}, bf16[400,128]{1,0:T(8,128)(2,1)S(1)}, u32[]{:S(2)}, u32[]{:S(2)}) collective-permute-start(bf16[400,128]{1,0:T(8,128)(2,1)S(1)} %pack.1.after_ref), channel_id=1, source_target_pairs={{0,4},{4,0},{1,5},{5,1},{2,6},{6,2},{3,7},{7,3},{8,12},{12,8},{9,1... | collective-permute-start | bytes 307208 | tf_op jit(solution)/shard_map/ppermute | solution.py:497
  9.2 4.8 %collective-permute-start.1 = (bf16[416,128]{1,0:T(8,128)(2,1)S(1)}, bf16[416,128]{1,0:T(8,128)(2,1)S(1)}, u32[]{:S(2)}, u32[]{:S(2)}) collective-permute-start(bf16[416,128]{1,0:T(8,128)(2,1)S(1)} %bitcast.8), channel_id=1, source_target_pairs={{0,4},{4,0},{1,5},{5,1},{2,6},{6,2},{3,7},{7,3},{8,12},{12,8},{9,1... | collective-permute-start | bytes 319496 | tf_op jit(solution)/shard_map/ppermute | solution.py:497

commit v4 on v3

v4 whole, which is shorter than its diff:
```python
import functools

import jax
import jax.numpy as jnp
from jax import lax
from jax.experimental import pallas as pl
from jax.experimental.pallas import tpu as pltpu
from jax.sharding import PartitionSpec as P

HEAD_SIZE = 64
LANES = 128
BLOCK = 64
NEG = -1e30
F32 = jnp.float32
BF16 = jnp.bfloat16
SCALE = HEAD_SIZE ** (-0.5)


def dot(left, right, left_dim, right_dim):
    return lax.dot_general(
        left, right, (((left_dim,), (right_dim,)), ((), ())), preferred_element_type=F32
    )


def join(parts, axis=0):
    return parts[0] if len(parts) == 1 else jnp.concatenate(parts, axis=axis)


class Sizes:
    def __init__(self, queries, keys, ctx_size):
        self.length = queries.shape[0]
        self.kv_heads = keys.shape[1] // HEAD_SIZE
        self.pairs = queries.shape[1] // keys.shape[1] // 2
        self.width = self.pairs * BLOCK
        self.blocks = self.length // BLOCK
        self.remote = ctx_size - 1
        self.cols = keys.shape[1]
        self.near = 2 * BLOCK * self.blocks * (self.blocks + 1) // 2
        self.stats = self.kv_heads * self.blocks * 2
        self.seg_rows = -(-self.length // LANES)
        self.slices = self.width // LANES
        self.extra = 3 * self.slices * 2 * self.kv_heads
        self.tall = 2 * self.length + -(-self.extra // 16) * 16

    def near_at(self, block):
        return slice(BLOCK * block * (block + 1), BLOCK * (block + 1) * (block + 2))

    def stat(self, head, block, half):
        return (head * self.blocks + block) * 2 + half

    def rows(self, block):
        return slice(block * BLOCK, (block + 1) * BLOCK)

    def lanes(self, head, pair):
        at = (head * self.pairs + pair) * LANES
        return slice(at, at + LANES)

    def span(self, head):
        at = head // 2 * LANES
        return slice(at, at + LANES)


def columns(row):
    return jnp.broadcast_to(row, (LANES, row.shape[1])).T


def split_halves(block, local):
    lane = lax.broadcasted_iota(jnp.int32, block.shape, 1)
    wide = block.astype(F32)
    turned = pltpu.roll(wide, HEAD_SIZE, 1)
    low = lane < HEAD_SIZE
    zero = jnp.zeros_like(wide)
    if local == 0:
        parts = (jnp.where(low, wide, zero), jnp.where(low, zero, turned))
    else:
        parts = (jnp.where(low, turned, zero), jnp.where(low, zero, wide))
    return [part.astype(BF16) for part in parts]


def seg_features(seg_col, blocked):
    lane = lax.broadcasted_iota(jnp.int32, seg_col.shape, 1)
    other = (lane - BLOCK) != seg_col.astype(jnp.int32)
    if blocked is not None:
        other = other | blocked
    return jnp.where((lane >= BLOCK) & other, NEG, 0.0)


def merge_heads(parts):
    lane = lax.broadcasted_iota(jnp.int32, parts[0][0].shape, 1)
    low = lane < HEAD_SIZE
    (first_low, first_high), (second_low, second_high) = parts
    straight = jnp.where(low, first_low, second_high)
    crossed = jnp.where(low, second_low, first_high)
    return straight + pltpu.roll(crossed, HEAD_SIZE, 1)


def halves(array):
    size = array.shape[0] // 2
    return array[:size], array[size:]


def fold(array, reduce):
    return reduce(array.reshape(array.shape[0] // 8, 8, array.shape[1]), axis=0)


def row_sum(tile):
    return jnp.sum(tile, axis=0, keepdims=True)


def row_max(tile):
    return jnp.max(tile, axis=0, keepdims=True)


def spread(pair_of_rows, size):
    width = pair_of_rows[0].shape[1]
    return join([jnp.broadcast_to(r, (size, width)) for r in pair_of_rows])


def sink_row(sz, sink_ref, head, half):
    lane = lax.broadcasted_iota(jnp.int32, (1, sz.width), 1)
    line = jnp.zeros((1, sz.width), F32)
    for pair in range(sz.pairs):
        value = sink_ref[head * 2 * sz.pairs + 2 * pair + half]
        line = jnp.where(lane // BLOCK == pair, value, line)
    return line


def pack_kernel(
    sz, ctx_axis, k_ref, v_ref, seg_ref, out_k_ref, out_v_ref, line_ref, k_sem, v_sem, seg_sem
):
    last = lax.axis_index(ctx_axis) == sz.remote

    @pl.when(last)
    def _():
        out_k_ref[...] = jnp.zeros_like(out_k_ref)
        out_v_ref[...] = jnp.zeros_like(out_v_ref)

    @pl.when(jnp.logical_not(last))
    def _():
        seg_copy = pltpu.make_async_copy(seg_ref, line_ref, seg_sem)
        k_copy = pltpu.make_async_copy(k_ref, out_k_ref.at[pl.ds(0, sz.length)], k_sem)
        v_copy = pltpu.make_async_copy(v_ref, out_v_ref, v_sem)
        seg_copy.start()
        k_copy.start()
        v_copy.start()
        seg_copy.wait()
        line = line_ref[...].astype(F32).astype(BF16)
        for i in range(sz.seg_rows):
            count = min(LANES, sz.length - i * LANES)
            at = sz.length + i
            out_k_ref[at : at + 1, :count] = line[:, i * LANES : i * LANES + count]
        k_copy.wait()
        v_copy.wait()


def seg_columns(sz, lines):
    lines = lines.astype(F32)
    parts = [columns(lines[i : i + 1, :LANES]) for i in range(sz.seg_rows)]
    return join(parts)[: sz.length]


def near_kernel(
    sz, q_hbm, k_hbm, v_hbm, g_hbm, seg_hbm, sink_hbm, after_k_ref, after_v_ref,
    q_ref, k_ref, g_ref, e_ref, dp_ref, top_ref, mass_ref, feat_ref, sink_rows_ref,
    q_flat, g_flat, v_ref, seg_ref, sink_ref, sems,
):
    del after_k_ref, after_v_ref
    pairs_of_refs = (
        (seg_hbm, seg_ref), (sink_hbm, sink_ref), (k_hbm, k_ref),
        (q_hbm, q_flat), (v_hbm, v_ref), (g_hbm, g_flat),
    )
    copies = [
        pltpu.make_async_copy(a, b, sems.at[i]) for i, (a, b) in enumerate(pairs_of_refs)
    ]
    for copy in copies:
        copy.start()

    def stack(ref, head, block):
        return join([ref[sz.rows(block), sz.lanes(head, pair)] for pair in range(sz.pairs)])

    shape = (sz.length, LANES)
    copies[0].wait()
    seg_col = columns(seg_ref[...].astype(F32))
    lane = lax.broadcasted_iota(jnp.int32, shape, 1)
    inner = lax.broadcasted_iota(jnp.int32, shape, 0) % BLOCK
    key_seg = seg_features(seg_col, None)
    key_plain = key_seg.astype(BF16)
    key_diag = jnp.where(lane == inner, 1.0, key_seg).astype(BF16)
    same = (lane - BLOCK) == seg_col.astype(jnp.int32)
    query_feat = jnp.where(
        lane < BLOCK, jnp.where(lane > inner, NEG, 0.0), jnp.where(same, 1.0, 0.0)
    ).astype(BF16)
    feat_ref[...] = query_feat
    for copy in copies[1:]:
        copy.wait()

    for head in range(sz.kv_heads):
        keys = split_halves(k_ref[:, sz.span(head)].astype(F32) * SCALE, head % 2)
        values = split_halves(v_ref[:, sz.span(head)], head % 2)
        sinks = [sink_row(sz, sink_ref, head, half) for half in range(2)]
        for half in range(2):
            sink_rows_ref[2 * head + half : 2 * head + half + 1] = sinks[half]
        for block in range(sz.blocks):
            count = (block + 1) * BLOCK
            rows = sz.rows(block)
            q_stack = stack(q_flat, head, block)
            q_ref[head, block] = q_stack
            q_wide = join([q_stack, join([query_feat[rows]] * sz.pairs)], 1)
            feats = join(([key_plain[: count - BLOCK]] if block else []) + [key_diag[rows]])
            key_wide = join([join([part[:count] for part in keys]), join([feats, feats])], 1)
            scores = dot(key_wide, q_wide, 1, 1)
            tops = [
                jnp.maximum(row_max(fold(part, jnp.max)), sinks[half])
                for half, part in enumerate(halves(scores))
            ]
            weight = jnp.exp(scores - spread(tops, count))
            at = sz.near_at(block)
            e_ref[head, at] = weight
            for half, part in enumerate(halves(weight)):
                r = sz.stat(head, block, half)
                top_ref[r : r + 1] = tops[half]
                mass_ref[r : r + 1] = jnp.exp(sinks[half] - tops[half]) + row_sum(
                    fold(part, jnp.sum)
                )
            g_stack = stack(g_flat, head, block)
            g_ref[head, block] = g_stack
            dp_ref[head, at] = dot(join([part[:count] for part in values]), g_stack, 1, 1)


def far_features(sz, far_k_ref, tile):
    seg_col = seg_columns(sz, far_k_ref[tile, sz.length :])
    feats = seg_features(seg_col, None).astype(BF16)
    return join([feats, feats])


def far_scores(sz, far_k_ref, q_ref, query_feat, head, block, tile, feats):
    keys = split_halves(far_k_ref[tile, : sz.length, sz.span(head)].astype(F32) * SCALE, head % 2)
    q_wide = join([q_ref[head, block], join([query_feat[sz.rows(block)]] * sz.pairs)], 1)
    return dot(join([join(keys), feats], 1), q_wide, 1, 1)


def stat_kernel(
    sz, ctx_axis, q_ref, far_k_ref, sink_rows_ref, top_ref, mass_ref, feat_ref,
    e_far_ref, top_out_ref, ratio_ref, inverse_ref, sink_prob_ref,
):
    place = lax.axis_index(ctx_axis)
    query_feat = feat_ref[...]

    def finish(head, block, half, top, mass):
        r = sz.stat(head, block, half)
        inverse = 1.0 / mass
        top_out_ref[r : r + 1] = top
        inverse_ref[r : r + 1] = inverse
        ratio_ref[r : r + 1] = jnp.exp(top_ref[r : r + 1] - top) * inverse
        sink = sink_rows_ref[2 * head + half : 2 * head + half + 1]
        sink_prob_ref[r : r + 1] = jnp.exp(sink - top) * inverse

    def each(body):
        for head in range(sz.kv_heads):
            for block in range(sz.blocks):
                body(head, block, [sz.stat(head, block, half) for half in range(2)])

    def inline():
        feats = far_features(sz, far_k_ref, 0)

        def body(head, block, stat):
            scores = far_scores(sz, far_k_ref, q_ref, query_feat, head, block, 0, feats)
            near_tops = [top_ref[r : r + 1] for r in stat]
            tops = [
                jnp.maximum(near, row_max(fold(part, jnp.max)))
                for near, part in zip(near_tops, halves(scores))
            ]
            weight = jnp.exp(scores - spread(tops, sz.length))
            e_far_ref[head, block] = weight
            for half, part in enumerate(halves(weight)):
                shrunk = mass_ref[stat[half] : stat[half] + 1] * jnp.exp(
                    near_tops[half] - tops[half]
                )
                finish(head, block, half, tops[half], shrunk + row_sum(fold(part, jnp.sum)))

        each(body)

    def looped(count):
        def body(head, block, stat):
            def step(tile, carry):
                feats = far_features(sz, far_k_ref, tile)
                scores = far_scores(sz, far_k_ref, q_ref, query_feat, head, block, tile, feats)
                tops, masses = carry
                new = tuple(
                    jnp.maximum(old, row_max(part)) for old, part in zip(tops, halves(scores))
                )
                weight = jnp.exp(scores - spread(new, sz.length))
                return new, tuple(
                    mass * jnp.exp(old - top) + row_sum(part)
                    for mass, old, top, part in zip(masses, tops, new, halves(weight))
                )

            start = (
                tuple(top_ref[r : r + 1] for r in stat),
                tuple(mass_ref[r : r + 1] for r in stat),
            )
            tops, masses = lax.fori_loop(0, count, step, start)
            for half in range(2):
                finish(head, block, half, tops[half], masses[half])

        each(body)

    if sz.remote == 1:

        @pl.when(place > 0)
        def _():
            inline()

        @pl.when(place == 0)
        def _():
            looped(0)

    else:
        looped(place)


def far_kernel(
    sz, ctx_axis, q_ref, g_ref, far_k_ref, far_v_ref, e_ref, dp_ref, feat_ref,
    e_far_ref, top_ref, ratio_ref, inverse_ref, sink_prob_ref,
    part_ref, ds_ref, delta_ref, sinks_out_ref,
    s_keep, dp_keep, p_keep,
):
    length, remote = sz.length, sz.remote
    place = lax.axis_index(ctx_axis)
    query_feat = feat_ref[...]

    def near_delta(head, block, ratio):
        at = sz.near_at(block)
        rounded = (e_ref[head, at] * spread(ratio, (block + 1) * BLOCK)).astype(BF16)
        prod = rounded.astype(F32) * dp_ref[head, at]
        return tuple(fold(part, jnp.sum) for part in halves(prod))

    def rows_of(ref, head, block):
        return [ref[r : r + 1] for r in (sz.stat(head, block, half) for half in range(2))]

    def finish(head, block, delta, sink_sums):
        for half, sink_prob in enumerate(rows_of(sink_prob_ref, head, block)):
            r = sz.stat(head, block, half)
            delta_ref[r : r + 1] = delta[half]
            sink_sums[half] = sink_sums[half] - sink_prob * delta[half]

    def put_sinks(head, sink_sums):
        for half in range(2):
            sinks_out_ref[2 * head + half : 2 * head + half + 1, :] = sink_sums[half]

    def values_of(head, tile):
        return join(split_halves(far_v_ref[tile, :, sz.span(head)], head % 2))

    def inline():
        sums = {}
        for head in range(sz.kv_heads):
            values = values_of(head, 0)
            sink_sums = [0.0, 0.0]
            p_far, ds_far = [], []
            for block in range(sz.blocks):
                delta = near_delta(head, block, rows_of(ratio_ref, head, block))
                dprob = dot(values, g_ref[head, block], 1, 1)
                prob = e_far_ref[head, block] * spread(rows_of(inverse_ref, head, block), length)
                rounded = prob.astype(BF16)
                p_far.append(rounded)
                delta = [
                    row_sum(near + fold(part, jnp.sum))
                    for near, part in zip(delta, halves(rounded.astype(F32) * dprob))
                ]
                finish(head, block, delta, sink_sums)
                dscore = (prob * (dprob - spread(delta, length))).astype(BF16)
                ds_far.append(dscore)
                for j in range(sz.slices):
                    ds_ref[head, block, 0, j] = dscore[:, j * LANES : (j + 1) * LANES]
            put_sinks(head, sink_sums)
            for which, parts, ref in ((0, ds_far, q_ref), (1, p_far, g_ref)):
                right = join([ref[head, block] for block in range(sz.blocks)])
                sums[which, head % 2] = halves(dot(join(parts, 1), right, 1, 0))
            if head % 2 == 1:
                for which, factor in ((0, SCALE), (1, 1.0)):
                    merged = merge_heads([sums[which, 0], sums[which, 1]]) * factor
                    rows = slice(which * length, (which + 1) * length)
                    part_ref[0, rows, sz.span(head)] = merged.astype(BF16)

    def looped(count):
        part_ref[:, : 2 * length] = jnp.zeros_like(part_ref[:, : 2 * length])
        for head in range(sz.kv_heads):
            span, local = sz.span(head), head % 2
            sink_sums = [0.0, 0.0]
            for block in range(sz.blocks):
                delta = near_delta(head, block, rows_of(ratio_ref, head, block))
                delta = tuple(row_sum(part) for part in delta)
                tops = rows_of(top_ref, head, block)
                inverse = rows_of(inverse_ref, head, block)

                def prob_far(tile, carry):
                    feats = far_features(sz, far_k_ref, tile)
                    scores = far_scores(
                        sz, far_k_ref, q_ref, query_feat, head, block, tile, feats
                    )
                    prob = jnp.exp(scores - spread(tops, length)) * spread(inverse, length)
                    rounded = prob.astype(BF16)
                    dprob = dot(values_of(head, tile), g_ref[head, block], 1, 1)
                    s_keep[tile] = prob
                    dp_keep[tile] = dprob
                    p_keep[block, tile] = rounded
                    return tuple(
                        c + row_sum(part)
                        for c, part in zip(carry, halves(rounded.astype(F32) * dprob))
                    )

                if remote > 1:
                    delta = lax.fori_loop(0, count, prob_far, delta)
                finish(head, block, delta, sink_sums)

                def dscore_far(tile, carry):
                    dscore = (s_keep[tile] * (dp_keep[tile] - spread(delta, length))).astype(BF16)
                    for j in range(sz.slices):
                        ds_ref[head, block, tile, j] = dscore[:, j * LANES : (j + 1) * LANES]
                    return carry

                if remote > 1:
                    lax.fori_loop(0, count, dscore_far, 0)
            put_sinks(head, sink_sums)

            def far_sum(tile, carry):
                for which, ref in ((0, q_ref), (1, g_ref)):
                    total = jnp.zeros((2 * length, LANES), F32)
                    for block in range(sz.blocks):
                        left = p_keep[block, tile]
                        if which == 0:
                            left = join([ds_ref[head, block, tile, j] for j in range(sz.slices)], 1)
                        total = total + dot(left, ref[head, block], 1, 0)
                    at = slice(which * length, (which + 1) * length)
                    lane = lax.broadcasted_iota(jnp.int32, (length, LANES), 1)
                    low = lane < HEAD_SIZE
                    a, b = halves(total)
                    turned = pltpu.roll(jnp.where(low, a, b), HEAD_SIZE, 1)
                    both = ((a if local == 0 else b) + turned) * (SCALE if which == 0 else 1.0)
                    keep = low if local == 0 else ~low
                    part_ref[tile, at, span] = jnp.where(
                        keep, both.astype(BF16), part_ref[tile, at, span]
                    )
                return carry

            if remote > 1:
                lax.fori_loop(0, count, far_sum, 0)

    if remote == 1:

        @pl.when(place > 0)
        def _():
            inline()

        @pl.when(place == 0)
        def _():
            looped(0)
            ds_ref[...] = jnp.zeros_like(ds_ref)

    else:
        looped(place)

    rest = sinks_out_ref[...]
    for i in range(3):
        piece = rest.astype(BF16)
        rest = rest - piece.astype(F32)
        for tile in range(remote):
            for j in range(sz.slices):
                at = 2 * length + 2 * sz.kv_heads * (i * sz.slices + j)
                part_ref[tile, at : at + 2 * sz.kv_heads, :LANES] = piece[
                    :, j * LANES : (j + 1) * LANES
                ]


def grad_kernel(
    sz, ctx_axis, q_ref, k_ref, g_ref, far_k_ref, e_ref, dp_ref, ratio_ref, delta_ref, ds_ref,
    dq_ref, own_ref,
):
    length, remote = sz.length, sz.remote
    place = lax.axis_index(ctx_axis)
    sums = {}
    for head in range(sz.kv_heads):
        span, local = sz.span(head), head % 2
        keys = split_halves(k_ref[:, span].astype(F32) * SCALE, local)
        p_near, ds_near, q_rows, g_rows = [], [], [], []

        def far_keys(tile):
            return join(split_halves(far_k_ref[tile, :length, span].astype(F32) * SCALE, local))

        if remote == 1:
            keys_here = far_keys(0)

        for block in range(sz.blocks):
            count = (block + 1) * BLOCK
            at = sz.near_at(block)
            q_rows.append(q_ref[head, block])
            g_rows.append(g_ref[head, block])
            stat = [sz.stat(head, block, half) for half in range(2)]
            ratio = [ratio_ref[r : r + 1] for r in stat]
            delta = [delta_ref[r : r + 1] for r in stat]
            prob = e_ref[head, at] * spread(ratio, count)
            p_near.append(prob.astype(BF16))
            dscore = (prob * (dp_ref[head, at] - spread(delta, count))).astype(BF16)
            ds_near.append(dscore)
            dq = dot(dscore, join([part[:count] for part in keys]), 0, 0)

            def ds_far(tile):
                return join([ds_ref[head, block, tile, j] for j in range(sz.slices)], 1)

            if remote == 1:
                dq = dq + dot(ds_far(0), keys_here, 0, 0)
            else:
                dq = lax.fori_loop(
                    0, place, lambda tile, c: c + dot(ds_far(tile), far_keys(tile), 0, 0), dq
                )
            for pair in range(sz.pairs):
                dq_ref[sz.rows(block), sz.lanes(head, pair)] = dq[
                    pair * BLOCK : (pair + 1) * BLOCK
                ].astype(BF16)

        for which, parts, right in ((0, ds_near, q_rows), (1, p_near, g_rows)):
            out = [[], []]
            for kb in range(sz.blocks):
                left = []
                for block in range(kb, sz.blocks):
                    left.append(join([half[sz.rows(kb)] for half in halves(parts[block])]))
                for half, total in enumerate(halves(dot(join(left, 1), join(right[kb:]), 1, 0))):
                    out[half].append(total)
            sums[which, local] = [join(o) for o in out]
        if local == 1:
            own_ref[0, :, span] = merge_heads([sums[0, 0], sums[0, 1]]) * SCALE
            own_ref[1, :, span] = merge_heads([sums[1, 0], sums[1, 1]])


def last_kernel(sz, own_ref, back_ref, sinks_ref, dk_ref, dv_ref, out_ref):
    length = sz.length
    totals = [own_ref[0], own_ref[1]]
    sink = sinks_ref[...]
    count = sink.shape[0]
    for tile in range(sz.remote):
        for which in range(2):
            at = slice(which * length, (which + 1) * length)
            totals[which] = totals[which] + back_ref[tile, at].astype(F32)
        rest = jnp.zeros_like(sink)
        for i in range(3):
            pieces = []
            for j in range(sz.slices):
                at = 2 * length + count * (i * sz.slices + j)
                pieces.append(back_ref[tile, at : at + count, :LANES].astype(F32))
            rest = rest + join(pieces, 1)
        sink = sink + rest
    dk_ref[...] = totals[0].astype(BF16)
    dv_ref[...] = totals[1].astype(BF16)
    lane = lax.broadcasted_iota(jnp.int32, sink.shape, 1)
    out_lane = lax.broadcasted_iota(jnp.int32, out_ref.shape, 1)
    line = jnp.zeros(out_ref.shape, F32)
    for pair in range(sz.pairs):
        sums = jnp.sum(jnp.where(lane // BLOCK == pair, sink, 0.0), axis=1, keepdims=True)
        for r in range(count):
            at = (r // 2) * 2 * sz.pairs + 2 * pair + r % 2
            line = jnp.where(out_lane == at, sums[r : r + 1], line)
    out_ref[...] = line


def on_device(ctx_size, queries, keys, values, grad_out, segments, sinks):
    sz = Sizes(queries, keys, ctx_size)
    length, width, remote = sz.length, sz.width, sz.remote
    vmem = pl.BlockSpec(memory_space=pltpu.VMEM)
    hbm = pl.BlockSpec(memory_space=pltpu.HBM)
    shape = jax.ShapeDtypeStruct
    seg_line = segments.reshape(1, length)
    small = remote == 1

    def stay(array):
        return pltpu.with_memory_space_constraint(array, pltpu.HBM)

    def params(mib):
        return pltpu.CompilerParams(vmem_limit_bytes=mib << 20)

    def cost(flops):
        return pl.CostEstimate(flops=flops, bytes_accessed=1 << 20, transcendentals=0)

    tile_flops = 4 * queries.shape[0] * queries.shape[1] * length

    pack_k, pack_v = pl.pallas_call(
        functools.partial(pack_kernel, sz, "ctx"),
        name="pack",
        out_shape=(shape((length + 16, sz.cols), BF16), shape(values.shape, BF16)),
        in_specs=[hbm, hbm, hbm],
        out_specs=(vmem, vmem),
        scratch_shapes=[pltpu.VMEM((1, length), jnp.int32)] + [pltpu.SemaphoreType.DMA] * 3,
        compiler_params=params(4),
    )(stay(keys), stay(values), stay(seg_line))

    def turn(array, shift):
        order = [(i, (i + shift) % ctx_size) for i in range(ctx_size)]
        return lax.ppermute(array, "ctx", order)

    far_k = jnp.stack([turn(pack_k, s) for s in range(1, ctx_size)])
    far_v = jnp.stack([turn(pack_v, s) for s in range(1, ctx_size)])

    stacked = shape((sz.kv_heads, sz.blocks, width, LANES), BF16)
    tiles = shape((sz.kv_heads, sz.near, width), F32)
    stats = shape((sz.stats, width), F32)
    q_here, k_here, g_here, weights, dprob, tops, mass, feats, sink_in = pl.pallas_call(
        functools.partial(near_kernel, sz),
        name="near",
        out_shape=(
            stacked,
            shape(keys.shape, BF16),
            stacked,
            tiles,
            tiles,
            stats,
            stats,
            shape((length, LANES), BF16),
            shape((2 * sz.kv_heads, width), F32),
        ),
        in_specs=[hbm] * 6 + [vmem] * 2,
        out_specs=(vmem,) * 9,
        scratch_shapes=[
            pltpu.VMEM(queries.shape, BF16),
            pltpu.VMEM(grad_out.shape, BF16),
            pltpu.VMEM(values.shape, BF16),
            pltpu.VMEM((1, length), jnp.int32),
            pltpu.SMEM(sinks.shape, F32),
            pltpu.SemaphoreType.DMA((6,)),
        ],
        compiler_params=params(16),
        cost_estimate=cost(2 * tile_flops),
    )(*[stay(a) for a in (queries, keys, values, grad_out, seg_line, sinks)], pack_k, pack_v)

    far_rows = 2 * length if small else 8
    e_far, tops, ratio, inverse, sink_prob = pl.pallas_call(
        functools.partial(stat_kernel, sz, "ctx"),
        name="stat",
        out_shape=(shape((sz.kv_heads, sz.blocks, far_rows, width), F32),) + (stats,) * 4,
        in_specs=[vmem] * 6,
        out_specs=(vmem,) * 5,
        compiler_params=params(16),
        cost_estimate=cost(tile_flops),
    )(q_here, far_k, sink_in, tops, mass, feats)

    many = (8, LANES) if small else (remote, 2 * length, width)
    part, ds_far, delta, sink_rows = pl.pallas_call(
        functools.partial(far_kernel, sz, "ctx"),
        name="far",
        out_shape=(
            shape((remote, sz.tall, sz.cols), BF16),
            shape((sz.kv_heads, sz.blocks, remote, sz.slices, 2 * length, LANES), BF16),
            stats,
            shape((2 * sz.kv_heads, width), F32),
        ),
        in_specs=[vmem] * 12,
        out_specs=(vmem,) * 4,
        scratch_shapes=[
            pltpu.VMEM(many, F32),
            pltpu.VMEM(many, F32),
            pltpu.VMEM((16, LANES) if small else (sz.blocks,) + many, BF16),
        ],
        compiler_params=params(16 if small else 60),
        cost_estimate=cost(3 * tile_flops),
    )(
        q_here, g_here, far_k, far_v, weights, dprob, feats,
        e_far, tops, ratio, inverse, sink_prob,
    )

    back = jnp.stack([turn(part[s - 1], -s) for s in range(1, ctx_size)])

    dq, own = pl.pallas_call(
        functools.partial(grad_kernel, sz, "ctx"),
        name="grad",
        out_shape=(shape(queries.shape, BF16), shape((2,) + keys.shape, F32)),
        in_specs=[vmem] * 9,
        out_specs=(vmem, vmem),
        compiler_params=params(16 if small else 60),
        cost_estimate=cost(4 * tile_flops),
    )(q_here, k_here, g_here, far_k, weights, dprob, ratio, delta, ds_far)

    heads = sinks.shape[0]
    dk, dv, line = pl.pallas_call(
        functools.partial(last_kernel, sz),
        name="last",
        out_shape=(shape(keys.shape, BF16), shape(values.shape, BF16), shape((1, heads), F32)),
        in_specs=[vmem, vmem, vmem],
        out_specs=(vmem, vmem, vmem),
        compiler_params=params(8),
    )(own, back, sink_rows)
    return dq, dk, dv, line.reshape(heads)


def solution(mesh):
    rows = P(("dp", "ctx"), "tp")
    return jax.shard_map(
        functools.partial(on_device, mesh.shape["ctx"]),
        mesh=mesh,
        in_specs=(rows, rows, rows, rows, P(("dp", "ctx")), P("tp")),
        out_specs=(rows, rows, rows, P(("dp", "tp"))),
        check_vma=False,
    )
```

time: 14.8 us -> 14 us (0.946)
  Pallas kernels: 7.79 us -> 5.99 us
  starting transfers between devices: 3.85 us -> 4.46 us
  waiting for transfers between devices: 2.3 us -> 2.69 us
    pallas_call x1, Pallas kernels: 2.3 us -> 0.46 us  [on_device(): pl.pallas_call(functools.partial(far_kernel, sz, 'ctx'), name='far', out_...]
    ppermute x2 -> x3, starting transfers between devices: 3.85 us -> 4.46 us  [turn(): return lax.ppermute(array, 'ctx', order)]
    ppermute x2 -> x3, waiting for transfers between devices: 2.3 us -> 2.69 us  [turn(): return lax.ppermute(array, 'ctx', order)]
    pallas_call x1 -> x2, Pallas kernels: 2 us -> 2.01 us  [the longest x1 1.98 us: on_device(): pl.pallas_call(functools.partial(grad_kernel, sz, 'ctx'), name='grad', ou...]
  transfers between devices with their start and end apart: 2 -> 3, of which waited for: 2 -> 2; matrix products, arithmetic and copies ran while one was open for 0% -> 0% of each run, Pallas kernels for 27% -> 29%
where the time goes in v4:
time: 14 us; the launch traced here: 13.8 us
  Pallas kernels  5.99 us (43%)
  starting transfers between devices  4.46 us (32%)
  waiting for transfers between devices  2.69 us (19%)
  between operations  0.65 us (5%)
    ppermute x3, starting transfers between devices, turn(): return lax.ppermute(array, 'ctx', order)  4.46 us
    ppermute x3, waiting for transfers between devices, turn(): return lax.ppermute(array, 'ctx', order)  2.69 us
    pallas_call x1, Pallas kernels, on_device(): pl.pallas_call(functools.partial(near_kernel, sz), name='near', out_shape...  1.98 us
    pallas_call x1, Pallas kernels, on_device(): pl.pallas_call(functools.partial(grad_kernel, sz, 'ctx'), name='grad', ou...  1.98 us
    pallas_call x1, Pallas kernels, on_device(): pl.pallas_call(functools.partial(pack_kernel, sz, 'ctx'), name='pack', ou...  0.88 us
    pallas_call x1, Pallas kernels, on_device(): pl.pallas_call(functools.partial(last_kernel, sz), name='last', out_shape...  0.66 us
    pallas_call x1, Pallas kernels, on_device(): pl.pallas_call(functools.partial(far_kernel, sz, 'ctx'), name='far', out_...  0.46 us
  transfers between devices with their start and end apart: 3, of which 2 were waited for; matrix products, arithmetic and copies ran while one was open for 0% of the time, Pallas kernels for 29%

profile of v4, /device:TPU:0, one launch (start us, length us, event | category | flops | bytes accessed | tf_op | source)
XLA Modules:
  0.0 13.8 jit_solution(6835517231075276471)
XLA Ops:
  0.6 0.9 %pack.1 = (bf16[208,128]{1,0:T(8,128)(2,1)S(1)}, bf16[192,128]{1,0:T(8,128)(2,1)S(1)}) custom-call(bf16[192,128]{1,0:T(8,128)(2,1)} %k_hbm.1, bf16[192,128]{1,0:T(8,128)(2,1)} %v_hbm.1, s32[1,192]{1,0:T(1,128)} %bitcast.12), custom_call_target="tpu_custom_call" | custom-call | tf_op jit(solution)/shard_map/pack/pallas_call | solution.py:585
  1.5 2.2 %collective-permute-start = (bf16[208,128]{1,0:T(8,128)(2,1)S(1)}, bf16[208,128]{1,0:T(8,128)(2,1)S(1)}, u32[]{:S(2)}, u32[]{:S(2)}) collective-permute-start(bf16[208,128]{1,0:T(8,128)(2,1)S(1)} %get-tuple-element.29.after_k_ref), channel_id=1, source_target_pairs={{0,4},{4,0},{1,5},{5,1},{2,6},{6,2},{3,7},{7,3},{8,12},{12,8},{9,1... | collective-permute-start | bytes 159752 | tf_op jit(solution)/shard_map/ppermute | solution.py:597
  3.8 0.1 collective-permute-start.1
  3.8 2.0 %near.1 = (bf16[2,3,256,128]{3,2,1,0:T(8,128)(2,1)S(1)}, bf16[192,128]{1,0:T(8,128)(2,1)S(1)}, bf16[2,3,256,128]{3,2,1,0:T(8,128)(2,1)S(1)}, f32[2,768,256]{2,1,...) custom-call(bf16[192,1024]{1,0:T(8,128)(2,1)} %q_hbm.1, ...), custom_call_target="tpu_custom_call" | custom-call | flops 301989888 | bytes 1048576 | tf_op jit(solution)/shard_map/near/pallas_call | solution.py:605
  5.8 0.0 collective-permute-done
  5.9 1.9 %collective-permute-done.1 = bf16[192,128]{1,0:T(8,128)(2,1)S(1)} collective-permute-done((bf16[192,128]{1,0:T(8,128)(2,1)S(1)}, bf16[192,128]{1,0:T(8,128)(2,1)S(1)}, u32[]{:S(2)}, u32[]{:S(2)}) %collective-permute-start.1) | collective-permute-done | bytes 49184 | tf_op jit(solution)/shard_map/ppermute | solution.py:597
  7.8 0.5 %far.1 = (bf16[1,416,128]{2,1,0:T(8,128)(2,1)S(1)}, bf16[2,3,1,2,384,128]{5,4,3,2,1,0:T(8,128)(2,1)S(1)}, f32[12,256]{1,0:T(8,128)S(1)}, f32[4,256]{1,0:T(4,128)S(1)}) custom-call(bf16[2,3,256,128]{3,2,1,0:T(8,128)(2,1)S(1)} %get-tuple-element.31.q_ref, bf16[2,3,256,128]{3,2,1,0:T(8,128)(2,1)S(1)} %get-tuple-element.33.g_ref, ...), custom_call_target="tpu_custom_call" | custom-call | flops 452984832 | bytes 1048576 | tf_op jit(solution)/shard_map/far/pallas_call | solution.py:645
  8.3 2.1 %collective-permute-start.2 = (bf16[416,128]{1,0:T(8,128)(2,1)S(1)}, bf16[416,128]{1,0:T(8,128)(2,1)S(1)}, u32[]{:S(2)}, u32[]{:S(2)}) collective-permute-start(bf16[416,128]{1,0:T(8,128)(2,1)S(1)} %bitcast.11), channel_id=1, source_target_pairs={{0,4},{4,0},{1,5},{5,1},{2,6},{6,2},{3,7},{7,3},{8,12},{12,8},{9,1... | collective-permute-start | bytes 319496 | tf_op jit(solution)/shard_map/ppermute | solution.py:597
  10.5 2.0 %grad.1 = (bf16[192,1024]{1,0:T(8,128)(2,1)}, f32[2,192,128]{2,1,0:T(8,128)S(1)}) custom-call(bf16[2,3,256,128]{3,2,1,0:T(8,128)(2,1)S(1)} %get-tuple-element.31.q_ref, bf16[192,128]{1,0:T(8,128)(2,1)S(1)} %get-tuple-element.32.k_ref, bf16[2,3,256,128]{3,2,1,0:T(8,128)(2,1)S(1)} %get-tuple-element.33.g_ref, bf16[1,208,128]{2,1,0:T(8,128)(2,1)S(1)} %bitcast.8, ...), custom_call_target="tpu_custom_call" | custom-call | flops 603979776 | bytes 1048576 | tf_op jit(solution)/shard_map/grad/pallas_call | solution.py:670
  12.4 0.7 %collective-permute-done.2 = bf16[416,128]{1,0:T(8,128)(2,1)S(1)} collective-permute-done((bf16[416,128]{1,0:T(8,128)(2,1)S(1)}, bf16[416,128]{1,0:T(8,128)(2,1)S(1)}, u32[]{:S(2)}, u32[]{:S(2)}) %collective-permute-start.2) | collective-permute-done | bytes 106528 | tf_op jit(solution)/shard_map/ppermute | solution.py:597
  13.1 0.7 %last.1 = (bf16[192,128]{1,0:T(8,128)(2,1)}, bf16[192,128]{1,0:T(8,128)(2,1)}, f32[1,16]{1,0:T(1,128)}) custom-call(f32[2,192,128]{2,1,0:T(8,128)S(1)} %get-tuple-element.48.own_ref, bf16[1,416,128]{2,1,0:T(8,128)(2,1)S(1)} %bitcast.9, f32[4,256]{1,0:T(4,128)S(1)} %get-tuple-element.50.sinks_ref), custom_call_target="tpu_custom_call" | custom-call | tf_op jit(solution)/shard_map/last/pallas_call | solution.py:681
  (1 shorter events, 0.0 us)
Async XLA Ops:
  1.5 4.4 %collective-permute-start = (bf16[208,128]{1,0:T(8,128)(2,1)S(1)}, bf16[208,128]{1,0:T(8,128)(2,1)S(1)}, u32[]{:S(2)}, u32[]{:S(2)}) collective-permute-start(bf16[208,128]{1,0:T(8,128)(2,1)S(1)} %get-tuple-element.29.after_k_ref), channel_id=1, source_target_pairs={{0,4},{4,0},{1,5},{5,1},{2,6},{6,2},{3,7},{7,3},{8,12},{12,8},{9,1... | collective-permute-start | bytes 159752 | tf_op jit(solution)/shard_map/ppermute | solution.py:597
  3.8 4.1 %collective-permute-start.1 = (bf16[192,128]{1,0:T(8,128)(2,1)S(1)}, bf16[192,128]{1,0:T(8,128)(2,1)S(1)}, u32[]{:S(2)}, u32[]{:S(2)}) collective-permute-start(bf16[192,128]{1,0:T(8,128)(2,1)S(1)} %get-tuple-element.30.after_v_ref), channel_id=1, source_target_pairs={{0,4},{4,0},{1,5},{5,1},{2,6},{6,2},{3,7},{7,3},{8,12},{12,8},{9,1... | collective-permute-start | bytes 147464 | tf_op jit(solution)/shard_map/ppermute | solution.py:597
  8.3 4.8 %collective-permute-start.2 = (bf16[416,128]{1,0:T(8,128)(2,1)S(1)}, bf16[416,128]{1,0:T(8,128)(2,1)S(1)}, u32[]{:S(2)}, u32[]{:S(2)}) collective-permute-start(bf16[416,128]{1,0:T(8,128)(2,1)S(1)} %bitcast.11), channel_id=1, source_target_pairs={{0,4},{4,0},{1,5},{5,1},{2,6},{6,2},{3,7},{7,3},{8,12},{12,8},{9,1... | collective-permute-start | bytes 319496 | tf_op jit(solution)/shard_map/ppermute | solution.py:597
